TPU v7x, 128 devices: a whole 4x4x4 slice. The times are simulated.
128 devices in a mesh: data: 1, inner: 16 (over z, y), stage: 8 (over x, core).
Axes of the slice: x: 4, y: 4, z: 4, core: 2. Of those that a mesh axis runs over, the one named last changes fastest.
Arguments:
- x: bfloat16 [8, 512, 1536], P(('data', 'stage'), 'inner')
- g: bfloat16 [8, 512, 1536], P(('data', 'stage'), 'inner')
- w1: bfloat16 [1, 8, 1536, 6144], P(None, 'stage')
- w2: bfloat16 [1, 8, 6144, 1536], P(None, 'stage')
Outputs:
- output 1: bfloat16 [8, 512, 1536], P(('data', 'stage'), 'inner')
- output 2: bfloat16 [8, 512, 1536], P(('data', 'stage'), 'inner')
- output 3: float32 [1, 8, 1536, 6144], P('data', 'stage')
- output 4: float32 [1, 8, 6144, 1536], P('data', 'stage')
All inputs are finite; a program needn't handle non-finite values.
Results may differ from a plain program's by a relative error of at most 0.02.
Values are sent between devices in bfloat16 or wider.
A program may use at most 1 GiB of HBM per device.

v0:
```python
import jax
import jax.numpy as jnp
from jax import lax
from jax.sharding import PartitionSpec as P


def _gelu(t):
    return jax.nn.gelu(t, approximate=True)


def _fwd(h, w1, w2):
    z = jnp.dot(h, w1, preferred_element_type=jnp.float32)
    a = _gelu(z).astype(jnp.bfloat16)
    u = jnp.dot(a, w2, preferred_element_type=jnp.float32)
    return (h.astype(jnp.float32) + u).astype(jnp.bfloat16)


def _bwd(h, dh, w1, w2):
    z = jnp.dot(h, w1, preferred_element_type=jnp.float32)
    a32, gelu_vjp = jax.vjp(_gelu, z)
    a = a32.astype(jnp.bfloat16)
    dw2 = jnp.dot(a.T, dh, preferred_element_type=jnp.float32)
    da = jnp.dot(dh, w2.T, preferred_element_type=jnp.float32)
    dz = gelu_vjp(da)[0].astype(jnp.bfloat16)
    dw1 = jnp.dot(h.T, dz, preferred_element_type=jnp.float32)
    dh_prev = (dh.astype(jnp.float32) + jnp.dot(dz, w1.T, preferred_element_type=jnp.float32)).astype(jnp.bfloat16)
    return dh_prev, dw1, dw2


def solution(mesh):
    n_stage = mesh.shape["stage"]
    fwd_perm = [(i, (i + 1) % n_stage) for i in range(n_stage)]
    bwd_perm = [(i, (i - 1) % n_stage) for i in range(n_stage)]

    def body(x, g, w1, w2):
        p = lax.axis_index("stage")
        q = n_stage - 1 - p
        nv, k, d, f = w1.shape
        mb, bl, _ = x.shape
        m = mb * n_stage
        n_ticks = nv * m + n_stage - 1
        x_all = lax.all_gather(x, "stage", axis=0, tiled=True)
        g_all = lax.all_gather(g, "stage", axis=0, tiled=True)

        def slot(s):
            valid = (s >= 0) & (s < nv * m)
            sc = jnp.clip(s, 0, nv * m - 1)
            return valid, sc // m, sc % m

        def fwd_tick(carry, t):
            inc, buf, saved, y_all = carry
            ok_in, _, m_in = slot(t - n_stage)
            buf = buf.at[m_in].set(jnp.where(ok_in & (p == 0), inc, buf[m_in]))
            ok, v, mi = slot(t - p)
            h = jnp.where(p == 0, jnp.where(v == 0, x_all[mi], buf[mi]), inc)
            w1v, w2v = w1[v], w2[v]
            hs = []
            for j in range(k):
                hs.append(h)
                h = _fwd(h, w1v[j], w2v[j])
            saved = saved.at[v, mi].set(jnp.where(ok, jnp.stack(hs), saved[v, mi]))
            last = ok & (p == n_stage - 1) & (v == nv - 1)
            y_all = y_all.at[mi].set(jnp.where(last, h, y_all[mi]))
            inc = lax.ppermute(h, "stage", fwd_perm)
            return (inc, buf, saved, y_all), None

        act0 = jnp.zeros((bl, d), jnp.bfloat16)
        per_mb0 = jnp.zeros((m, bl, d), jnp.bfloat16)
        saved0 = jnp.zeros((nv, m, k, bl, d), jnp.bfloat16)
        ticks = jnp.arange(n_ticks, dtype=jnp.int32)
        (_, _, saved, y_all), _ = lax.scan(fwd_tick, (act0, per_mb0, saved0, per_mb0), ticks)

        def bwd_tick(carry, t):
            inc, buf, dw1, dw2, dx_all = carry
            ok_in, _, m_in = slot(t - n_stage)
            buf = buf.at[m_in].set(jnp.where(ok_in & (q == 0), inc, buf[m_in]))
            ok, u, mi = slot(t - q)
            v = nv - 1 - u
            dh = jnp.where(q == 0, jnp.where(u == 0, g_all[mi], buf[mi]), inc)
            hs = saved[v, mi]
            w1v, w2v = w1[v], w2[v]
            d1s = [None] * k
            d2s = [None] * k
            for j in reversed(range(k)):
                dh, d1s[j], d2s[j] = _bwd(hs[j], dh, w1v[j], w2v[j])
            on = ok.astype(jnp.float32)
            dw1 = dw1.at[v].add(jnp.stack(d1s) * on)
            dw2 = dw2.at[v].add(jnp.stack(d2s) * on)
            first = ok & (p == 0) & (v == 0)
            dx_all = dx_all.at[mi].set(jnp.where(first, dh, dx_all[mi]))
            inc = lax.ppermute(dh, "stage", bwd_perm)
            return (inc, buf, dw1, dw2, dx_all), None

        dw1_0 = jnp.zeros((nv, k, d, f), jnp.float32)
        dw2_0 = jnp.zeros((nv, k, f, d), jnp.float32)
        (_, _, dw1, dw2, dx_all), _ = lax.scan(bwd_tick, (act0, per_mb0, dw1_0, dw2_0, per_mb0), ticks)

        zero = jnp.zeros_like(y_all)
        y = lax.psum_scatter(jnp.where(p == n_stage - 1, y_all, zero), "stage", scatter_dimension=0, tiled=True)
        dx = lax.psum_scatter(jnp.where(p == 0, dx_all, zero), "stage", scatter_dimension=0, tiled=True)
        dw1 = lax.psum(dw1, "inner")
        dw2 = lax.psum(dw2, "inner")
        return y, dx, dw1, dw2

    tok = P(("data", "stage"), "inner", None)
    wsp = P(None, "stage", None, None)
    dsp = P("data", "stage", None, None)
    return jax.shard_map(body, mesh=mesh, in_specs=(tok, tok, wsp, wsp), out_specs=(tok, tok, dsp, dsp), check_vma=False)
```

profile of v0, /device:TPU:0, one launch (start us, length us, event | category | flops | bytes accessed | tf_op | source)
XLA Modules:
  0.0 2759.1 jit_solution(17947792340898630912)
XLA Ops:
  22.2 420.2 %while.46 = (s32[]{:T(128)}, bf16[32,1536]{1,0:T(8,128)(2,1)S(1)}, bf16[8,32,1536]{2,1,0:T(8,128)(2,1)S(1)}, bf16[1,8,1,32,1536]{4,3,2,1,0:T(8,128)(2,1)S(1)}, b...) while((s32[]{:T(128)}, bf16[32,1536]{1,0:T(8,128)(2,1)S(1)}, ...), condition=%wide.region_4.5_spmd, body=%wide.region_0.4_spmd.sunk | while | flops 1210269824 | bytes 40108828 | solution.py:71
  457.1 1426.1 %while.47 = (s32[]{:T(128)}, bf16[32,1536]{1,0:T(8,128)(2,1)S(1)}, bf16[8,32,1536]{2,1,0:T(8,128)(2,1)S(1)}, f32[1,1,1536,6144]{3,2,1,0:T(8,128)}, f32[1,1,6144,...) while((s32[]{:T(128)}, bf16[32,1536]{1,0:T(8,128)(2,1)S(1)}, ...), condition=%wide.region_10.11_spmd.clone, body=%wide.region_6.10_spmd.clone.sunk | while | flops 3101540352 | bytes 219711824 | solution.py:96
  567.3 28.4 %add_select_fusion.5 = f32[1,1,6144,1536]{3,2,1,0:T(8,128)} fusion(f32[1,1,6144,1536]{3,2,1,0:T(8,128)} %get-tuple-element.802, bf16[32,1536]{1,0:T(8,128)(2,1)S(1)} %bitcast_select_fusion.14, f32[]{:T(128)S(6)} %convert_element_type.72, pred[]{:T(512)S(6)} %compare.140, pred[]{:T(512)} %and_reduce_fusion.13, f32[32,6144]{1,0:T(8,128)S(1)} %fusion.110), kind=kOutput, calls=%fused_computation.43.clone.1 | convolution fusion | flops 643497984 | bytes 76382216 | tf_op jit(solution)/shard_map/while/body/eval_jaxpr/dot_general | solution.py:22
  595.7 28.4 %add_select_fusion.4 = f32[1,1,1536,6144]{3,2,1,0:T(8,128)} fusion(f32[1,1,1536,6144]{3,2,1,0:T(8,128)} %get-tuple-element.801, bf16[32,6144]{1,0:T(8,128)(2,1)S(1)} %fusion.111, f32[]{:T(128)S(6)} %convert_element_type.72, pred[]{:T(512)S(6)} %compare.140, pred[]{:T(512)} %and_reduce_fusion.13, ...), kind=kOutput, calls=%fused_computation.44.clone.1 | convolution fusion | flops 641728512 | bytes 75989000 | tf_op jit(solution)/shard_map/while/body/eval_jaxpr/dot_general | solution.py:25
  693.3 28.4 %add_select_fusion.4 = f32[1,1,1536,6144]{3,2,1,0:T(8,128)} fusion(f32[1,1,1536,6144]{3,2,1,0:T(8,128)} %get-tuple-element.801, bf16[32,6144]{1,0:T(8,128)(2,1)S(1)} %fusion.111, f32[]{:T(128)S(6)} %convert_element_type.72, pred[]{:T(512)S(6)} %compare.140, pred[]{:T(512)} %and_reduce_fusion.13, ...), kind=kOutput, calls=%fused_computation.44.clone.1 | convolution fusion | flops 641728512 | bytes 75989000 | tf_op jit(solution)/shard_map/while/body/eval_jaxpr/dot_general | solution.py:25
  761.3 28.4 %add_select_fusion.5 = f32[1,1,6144,1536]{3,2,1,0:T(8,128)} fusion(f32[1,1,6144,1536]{3,2,1,0:T(8,128)} %get-tuple-element.802, bf16[32,1536]{1,0:T(8,128)(2,1)S(1)} %bitcast_select_fusion.14, f32[]{:T(128)S(6)} %convert_element_type.72, pred[]{:T(512)S(6)} %compare.140, pred[]{:T(512)} %and_reduce_fusion.13, f32[32,6144]{1,0:T(8,128)S(1)} %fusion.110), kind=kOutput, calls=%fused_computation.43.clone.1 | convolution fusion | flops 643497984 | bytes 76382216 | tf_op jit(solution)/shard_map/while/body/eval_jaxpr/dot_general | solution.py:22
  789.7 28.4 %add_select_fusion.4 = f32[1,1,1536,6144]{3,2,1,0:T(8,128)} fusion(f32[1,1,1536,6144]{3,2,1,0:T(8,128)} %get-tuple-element.801, bf16[32,6144]{1,0:T(8,128)(2,1)S(1)} %fusion.111, f32[]{:T(128)S(6)} %convert_element_type.72, pred[]{:T(512)S(6)} %compare.140, pred[]{:T(512)} %and_reduce_fusion.13, ...), kind=kOutput, calls=%fused_computation.44.clone.1 | convolution fusion | flops 641728512 | bytes 75989000 | tf_op jit(solution)/shard_map/while/body/eval_jaxpr/dot_general | solution.py:25
  857.4 28.4 %add_select_fusion.5 = f32[1,1,6144,1536]{3,2,1,0:T(8,128)} fusion(f32[1,1,6144,1536]{3,2,1,0:T(8,128)} %get-tuple-element.802, bf16[32,1536]{1,0:T(8,128)(2,1)S(1)} %bitcast_select_fusion.14, f32[]{:T(128)S(6)} %convert_element_type.72, pred[]{:T(512)S(6)} %compare.140, pred[]{:T(512)} %and_reduce_fusion.13, f32[32,6144]{1,0:T(8,128)S(1)} %fusion.110), kind=kOutput, calls=%fused_computation.43.clone.1 | convolution fusion | flops 643497984 | bytes 76382216 | tf_op jit(solution)/shard_map/while/body/eval_jaxpr/dot_general | solution.py:22
  885.9 28.4 %add_select_fusion.4 = f32[1,1,1536,6144]{3,2,1,0:T(8,128)} fusion(f32[1,1,1536,6144]{3,2,1,0:T(8,128)} %get-tuple-element.801, bf16[32,6144]{1,0:T(8,128)(2,1)S(1)} %fusion.111, f32[]{:T(128)S(6)} %convert_element_type.72, pred[]{:T(512)S(6)} %compare.140, pred[]{:T(512)} %and_reduce_fusion.13, ...), kind=kOutput, calls=%fused_computation.44.clone.1 | convolution fusion | flops 641728512 | bytes 75989000 | tf_op jit(solution)/shard_map/while/body/eval_jaxpr/dot_general | solution.py:25
  982.0 28.4 %add_select_fusion.4 = f32[1,1,1536,6144]{3,2,1,0:T(8,128)} fusion(f32[1,1,1536,6144]{3,2,1,0:T(8,128)} %get-tuple-element.801, bf16[32,6144]{1,0:T(8,128)(2,1)S(1)} %fusion.111, f32[]{:T(128)S(6)} %convert_element_type.72, pred[]{:T(512)S(6)} %compare.140, pred[]{:T(512)} %and_reduce_fusion.13, ...), kind=kOutput, calls=%fused_computation.44.clone.1 | convolution fusion | flops 641728512 | bytes 75989000 | tf_op jit(solution)/shard_map/while/body/eval_jaxpr/dot_general | solution.py:25
  1052.2 28.4 %add_select_fusion.5 = f32[1,1,6144,1536]{3,2,1,0:T(8,128)} fusion(f32[1,1,6144,1536]{3,2,1,0:T(8,128)} %get-tuple-element.802, bf16[32,1536]{1,0:T(8,128)(2,1)S(1)} %bitcast_select_fusion.14, f32[]{:T(128)S(6)} %convert_element_type.72, pred[]{:T(512)S(6)} %compare.140, pred[]{:T(512)} %and_reduce_fusion.13, f32[32,6144]{1,0:T(8,128)S(1)} %fusion.110), kind=kOutput, calls=%fused_computation.43.clone.1 | convolution fusion | flops 643497984 | bytes 76382216 | tf_op jit(solution)/shard_map/while/body/eval_jaxpr/dot_general | solution.py:22
  1080.6 28.4 %add_select_fusion.4 = f32[1,1,1536,6144]{3,2,1,0:T(8,128)} fusion(f32[1,1,1536,6144]{3,2,1,0:T(8,128)} %get-tuple-element.801, bf16[32,6144]{1,0:T(8,128)(2,1)S(1)} %fusion.111, f32[]{:T(128)S(6)} %convert_element_type.72, pred[]{:T(512)S(6)} %compare.140, pred[]{:T(512)} %and_reduce_fusion.13, ...), kind=kOutput, calls=%fused_computation.44.clone.1 | convolution fusion | flops 641728512 | bytes 75989000 | tf_op jit(solution)/shard_map/while/body/eval_jaxpr/dot_general | solution.py:25
  1148.5 28.4 %add_select_fusion.5 = f32[1,1,6144,1536]{3,2,1,0:T(8,128)} fusion(f32[1,1,6144,1536]{3,2,1,0:T(8,128)} %get-tuple-element.802, bf16[32,1536]{1,0:T(8,128)(2,1)S(1)} %bitcast_select_fusion.14, f32[]{:T(128)S(6)} %convert_element_type.72, pred[]{:T(512)S(6)} %compare.140, pred[]{:T(512)} %and_reduce_fusion.13, f32[32,6144]{1,0:T(8,128)S(1)} %fusion.110), kind=kOutput, calls=%fused_computation.43.clone.1 | convolution fusion | flops 643497984 | bytes 76382216 | tf_op jit(solution)/shard_map/while/body/eval_jaxpr/dot_general | solution.py:22
  1176.9 28.4 %add_select_fusion.4 = f32[1,1,1536,6144]{3,2,1,0:T(8,128)} fusion(f32[1,1,1536,6144]{3,2,1,0:T(8,128)} %get-tuple-element.801, bf16[32,6144]{1,0:T(8,128)(2,1)S(1)} %fusion.111, f32[]{:T(128)S(6)} %convert_element_type.72, pred[]{:T(512)S(6)} %compare.140, pred[]{:T(512)} %and_reduce_fusion.13, ...), kind=kOutput, calls=%fused_computation.44.clone.1 | convolution fusion | flops 641728512 | bytes 75989000 | tf_op jit(solution)/shard_map/while/body/eval_jaxpr/dot_general | solution.py:25
  1245.1 28.4 %add_select_fusion.5 = f32[1,1,6144,1536]{3,2,1,0:T(8,128)} fusion(f32[1,1,6144,1536]{3,2,1,0:T(8,128)} %get-tuple-element.802, bf16[32,1536]{1,0:T(8,128)(2,1)S(1)} %bitcast_select_fusion.14, f32[]{:T(128)S(6)} %convert_element_type.72, pred[]{:T(512)S(6)} %compare.140, pred[]{:T(512)} %and_reduce_fusion.13, f32[32,6144]{1,0:T(8,128)S(1)} %fusion.110), kind=kOutput, calls=%fused_computation.43.clone.1 | convolution fusion | flops 643497984 | bytes 76382216 | tf_op jit(solution)/shard_map/while/body/eval_jaxpr/dot_general | solution.py:22
  1273.5 28.4 %add_select_fusion.4 = f32[1,1,1536,6144]{3,2,1,0:T(8,128)} fusion(f32[1,1,1536,6144]{3,2,1,0:T(8,128)} %get-tuple-element.801, bf16[32,6144]{1,0:T(8,128)(2,1)S(1)} %fusion.111, f32[]{:T(128)S(6)} %convert_element_type.72, pred[]{:T(512)S(6)} %compare.140, pred[]{:T(512)} %and_reduce_fusion.13, ...), kind=kOutput, calls=%fused_computation.44.clone.1 | convolution fusion | flops 641728512 | bytes 75989000 | tf_op jit(solution)/shard_map/while/body/eval_jaxpr/dot_general | solution.py:25
  1369.9 28.4 %add_select_fusion.4 = f32[1,1,1536,6144]{3,2,1,0:T(8,128)} fusion(f32[1,1,1536,6144]{3,2,1,0:T(8,128)} %get-tuple-element.801, bf16[32,6144]{1,0:T(8,128)(2,1)S(1)} %fusion.111, f32[]{:T(128)S(6)} %convert_element_type.72, pred[]{:T(512)S(6)} %compare.140, pred[]{:T(512)} %and_reduce_fusion.13, ...), kind=kOutput, calls=%fused_computation.44.clone.1 | convolution fusion | flops 641728512 | bytes 75989000 | tf_op jit(solution)/shard_map/while/body/eval_jaxpr/dot_general | solution.py:25
  1467.6 28.4 %add_select_fusion.4 = f32[1,1,1536,6144]{3,2,1,0:T(8,128)} fusion(f32[1,1,1536,6144]{3,2,1,0:T(8,128)} %get-tuple-element.801, bf16[32,6144]{1,0:T(8,128)(2,1)S(1)} %fusion.111, f32[]{:T(128)S(6)} %convert_element_type.72, pred[]{:T(512)S(6)} %compare.140, pred[]{:T(512)} %and_reduce_fusion.13, ...), kind=kOutput, calls=%fused_computation.44.clone.1 | convolution fusion | flops 641728512 | bytes 75989000 | tf_op jit(solution)/shard_map/while/body/eval_jaxpr/dot_general | solution.py:25
  1563.9 28.4 %add_select_fusion.4 = f32[1,1,1536,6144]{3,2,1,0:T(8,128)} fusion(f32[1,1,1536,6144]{3,2,1,0:T(8,128)} %get-tuple-element.801, bf16[32,6144]{1,0:T(8,128)(2,1)S(1)} %fusion.111, f32[]{:T(128)S(6)} %convert_element_type.72, pred[]{:T(512)S(6)} %compare.140, pred[]{:T(512)} %and_reduce_fusion.13, ...), kind=kOutput, calls=%fused_computation.44.clone.1 | convolution fusion | flops 641728512 | bytes 75989000 | tf_op jit(solution)/shard_map/while/body/eval_jaxpr/dot_general | solution.py:25
  1660.1 28.4 %add_select_fusion.4 = f32[1,1,1536,6144]{3,2,1,0:T(8,128)} fusion(f32[1,1,1536,6144]{3,2,1,0:T(8,128)} %get-tuple-element.801, bf16[32,6144]{1,0:T(8,128)(2,1)S(1)} %fusion.111, f32[]{:T(128)S(6)} %convert_element_type.72, pred[]{:T(512)S(6)} %compare.140, pred[]{:T(512)} %and_reduce_fusion.13, ...), kind=kOutput, calls=%fused_computation.44.clone.1 | convolution fusion | flops 641728512 | bytes 75989000 | tf_op jit(solution)/shard_map/while/body/eval_jaxpr/dot_general | solution.py:25
  1756.3 28.4 %add_select_fusion.4 = f32[1,1,1536,6144]{3,2,1,0:T(8,128)} fusion(f32[1,1,1536,6144]{3,2,1,0:T(8,128)} %get-tuple-element.801, bf16[32,6144]{1,0:T(8,128)(2,1)S(1)} %fusion.111, f32[]{:T(128)S(6)} %convert_element_type.72, pred[]{:T(512)S(6)} %compare.140, pred[]{:T(512)} %and_reduce_fusion.13, ...), kind=kOutput, calls=%fused_computation.44.clone.1 | convolution fusion | flops 641728512 | bytes 75989000 | tf_op jit(solution)/shard_map/while/body/eval_jaxpr/dot_general | solution.py:25
  1854.8 28.4 %add_select_fusion.4 = f32[1,1,1536,6144]{3,2,1,0:T(8,128)} fusion(f32[1,1,1536,6144]{3,2,1,0:T(8,128)} %get-tuple-element.801, bf16[32,6144]{1,0:T(8,128)(2,1)S(1)} %fusion.111, f32[]{:T(128)S(6)} %convert_element_type.72, pred[]{:T(512)S(6)} %compare.140, pred[]{:T(512)} %and_reduce_fusion.13, ...), kind=kOutput, calls=%fused_computation.44.clone.1 | convolution fusion | flops 641728512 | bytes 75989000 | tf_op jit(solution)/shard_map/while/body/eval_jaxpr/dot_general | solution.py:25
  1884.8 32.6 %reduce-scatter.5.cloned.1.call-done = bf16[1,32,1536]{2,1,0:T(8,128)(2,1)} async-done(((bf16[8,32,1536]{2,1,0:T(8,128)(2,1)}), bf16[1,32,1536]{2,1,0:T(8,128)(2,1)}) %reduce-scatter.5.cloned.1.call-update) | async-done | bytes 98320 | tf_op jit(solution)/shard_map/reduce_scatter | solution.py:100
  1917.4 785.5 %all-reduce.3.cloned.1.call-done = (f32[1,1,1536,6144]{3,2,1,0:T(8,128)}, f32[1,1,6144,1536]{3,2,1,0:T(8,128)}) async-done(((f32[1,1,1536,6144]{3,2,1,0:T(8,128)}, f32[1,1,6144,1536]{3,2,1,0:T(8,128)}), (f32[1,1,1536,6144]{3,2,1,0:T(8,128)}, f32[1,1,6144,1536]{3,2,1,0:T(8,128)})) %all-reduce.3.cloned.1.call-update) | async-done | bytes 75497488 | tf_op jit(solution)/shard_map/psum | solution.py:101
  (428 shorter events, 1315.4 us)
Async XLA Ops:
  8.0 1876.8 %reduce-scatter.3.cloned.1.call-start = ((), (), s32[]{:S(2)}) async-start(), calls=%async_computation.2 | async-start | bytes 884736 | tf_op jit(solution)/shard_map/reduce_scatter | solution.py:99
  44.9 5.3 collective-permute-start
  72.9 5.3 collective-permute-start
  100.9 5.3 collective-permute-start
  129.0 5.3 collective-permute-start
  157.0 5.3 collective-permute-start
  213.0 5.3 collective-permute-start
  443.4 1474.0 %reduce-scatter.5.cloned.1.call-start = ((), (), s32[]{:S(2)}) async-start(), calls=%async_computation.3 | async-start | bytes 884736 | tf_op jit(solution)/shard_map/reduce_scatter | solution.py:100
  495.9 31.9 %collective-permute-start.1 = (bf16[32,1536]{1,0:T(8,128)(2,1)S(1)}, bf16[32,1536]{1,0:T(8,128)(2,1)S(1)}, u32[]{:S(2)}, u32[]{:S(2)}) collective-permute-start(bf16[32,1536]{1,0:T(8,128)(2,1)S(1)} %get-tuple-element.707), channel_id=1, source_target_pairs={{0,7},{1,0},{2,1},{3,2},{4,3},{5,4},{6,5},{7,6},{8,15},{9,8},{10,9... | collective-permute-start | bytes 294920 | tf_op jit(solution)/shard_map/while/body/eval_jaxpr/ppermute | solution.py:91
  566.3 57.9 %collective-permute-start.1 = (bf16[32,1536]{1,0:T(8,128)(2,1)S(1)}, bf16[32,1536]{1,0:T(8,128)(2,1)S(1)}, u32[]{:S(2)}, u32[]{:S(2)}) collective-permute-start(bf16[32,1536]{1,0:T(8,128)(2,1)S(1)} %get-tuple-element.707), channel_id=1, source_target_pairs={{0,7},{1,0},{2,1},{3,2},{4,3},{5,4},{6,5},{7,6},{8,15},{9,8},{10,9... | collective-permute-start | bytes 294920 | tf_op jit(solution)/shard_map/while/body/eval_jaxpr/ppermute | solution.py:91
  662.6 59.2 %collective-permute-start.1 = (bf16[32,1536]{1,0:T(8,128)(2,1)S(1)}, bf16[32,1536]{1,0:T(8,128)(2,1)S(1)}, u32[]{:S(2)}, u32[]{:S(2)}) collective-permute-start(bf16[32,1536]{1,0:T(8,128)(2,1)S(1)} %get-tuple-element.707), channel_id=1, source_target_pairs={{0,7},{1,0},{2,1},{3,2},{4,3},{5,4},{6,5},{7,6},{8,15},{9,8},{10,9... | collective-permute-start | bytes 294920 | tf_op jit(solution)/shard_map/while/body/eval_jaxpr/ppermute | solution.py:91
  760.3 57.9 %collective-permute-start.1 = (bf16[32,1536]{1,0:T(8,128)(2,1)S(1)}, bf16[32,1536]{1,0:T(8,128)(2,1)S(1)}, u32[]{:S(2)}, u32[]{:S(2)}) collective-permute-start(bf16[32,1536]{1,0:T(8,128)(2,1)S(1)} %get-tuple-element.707), channel_id=1, source_target_pairs={{0,7},{1,0},{2,1},{3,2},{4,3},{5,4},{6,5},{7,6},{8,15},{9,8},{10,9... | collective-permute-start | bytes 294920 | tf_op jit(solution)/shard_map/while/body/eval_jaxpr/ppermute | solution.py:91
  856.6 57.7 %collective-permute-start.1 = (bf16[32,1536]{1,0:T(8,128)(2,1)S(1)}, bf16[32,1536]{1,0:T(8,128)(2,1)S(1)}, u32[]{:S(2)}, u32[]{:S(2)}) collective-permute-start(bf16[32,1536]{1,0:T(8,128)(2,1)S(1)} %get-tuple-element.707), channel_id=1, source_target_pairs={{0,7},{1,0},{2,1},{3,2},{4,3},{5,4},{6,5},{7,6},{8,15},{9,8},{10,9... | collective-permute-start | bytes 294920 | tf_op jit(solution)/shard_map/while/body/eval_jaxpr/ppermute | solution.py:91
  952.8 57.7 %collective-permute-start.1 = (bf16[32,1536]{1,0:T(8,128)(2,1)S(1)}, bf16[32,1536]{1,0:T(8,128)(2,1)S(1)}, u32[]{:S(2)}, u32[]{:S(2)}) collective-permute-start(bf16[32,1536]{1,0:T(8,128)(2,1)S(1)} %get-tuple-element.707), channel_id=1, source_target_pairs={{0,7},{1,0},{2,1},{3,2},{4,3},{5,4},{6,5},{7,6},{8,15},{9,8},{10,9... | collective-permute-start | bytes 294920 | tf_op jit(solution)/shard_map/while/body/eval_jaxpr/ppermute | solution.py:91
  1049.0 60.1 %collective-permute-start.1 = (bf16[32,1536]{1,0:T(8,128)(2,1)S(1)}, bf16[32,1536]{1,0:T(8,128)(2,1)S(1)}, u32[]{:S(2)}, u32[]{:S(2)}) collective-permute-start(bf16[32,1536]{1,0:T(8,128)(2,1)S(1)} %get-tuple-element.707), channel_id=1, source_target_pairs={{0,7},{1,0},{2,1},{3,2},{4,3},{5,4},{6,5},{7,6},{8,15},{9,8},{10,9... | collective-permute-start | bytes 294920 | tf_op jit(solution)/shard_map/while/body/eval_jaxpr/ppermute | solution.py:91
  1147.5 57.9 %collective-permute-start.1 = (bf16[32,1536]{1,0:T(8,128)(2,1)S(1)}, bf16[32,1536]{1,0:T(8,128)(2,1)S(1)}, u32[]{:S(2)}, u32[]{:S(2)}) collective-permute-start(bf16[32,1536]{1,0:T(8,128)(2,1)S(1)} %get-tuple-element.707), channel_id=1, source_target_pairs={{0,7},{1,0},{2,1},{3,2},{4,3},{5,4},{6,5},{7,6},{8,15},{9,8},{10,9... | collective-permute-start | bytes 294920 | tf_op jit(solution)/shard_map/while/body/eval_jaxpr/ppermute | solution.py:91
  1243.9 58.1 %collective-permute-start.1 = (bf16[32,1536]{1,0:T(8,128)(2,1)S(1)}, bf16[32,1536]{1,0:T(8,128)(2,1)S(1)}, u32[]{:S(2)}, u32[]{:S(2)}) collective-permute-start(bf16[32,1536]{1,0:T(8,128)(2,1)S(1)} %get-tuple-element.707), channel_id=1, source_target_pairs={{0,7},{1,0},{2,1},{3,2},{4,3},{5,4},{6,5},{7,6},{8,15},{9,8},{10,9... | collective-permute-start | bytes 294920 | tf_op jit(solution)/shard_map/while/body/eval_jaxpr/ppermute | solution.py:91
  1340.5 57.9 %collective-permute-start.1 = (bf16[32,1536]{1,0:T(8,128)(2,1)S(1)}, bf16[32,1536]{1,0:T(8,128)(2,1)S(1)}, u32[]{:S(2)}, u32[]{:S(2)}) collective-permute-start(bf16[32,1536]{1,0:T(8,128)(2,1)S(1)} %get-tuple-element.707), channel_id=1, source_target_pairs={{0,7},{1,0},{2,1},{3,2},{4,3},{5,4},{6,5},{7,6},{8,15},{9,8},{10,9... | collective-permute-start | bytes 294920 | tf_op jit(solution)/shard_map/while/body/eval_jaxpr/ppermute | solution.py:91
  1436.8 59.2 %collective-permute-start.1 = (bf16[32,1536]{1,0:T(8,128)(2,1)S(1)}, bf16[32,1536]{1,0:T(8,128)(2,1)S(1)}, u32[]{:S(2)}, u32[]{:S(2)}) collective-permute-start(bf16[32,1536]{1,0:T(8,128)(2,1)S(1)} %get-tuple-element.707), channel_id=1, source_target_pairs={{0,7},{1,0},{2,1},{3,2},{4,3},{5,4},{6,5},{7,6},{8,15},{9,8},{10,9... | collective-permute-start | bytes 294920 | tf_op jit(solution)/shard_map/while/body/eval_jaxpr/ppermute | solution.py:91
  1534.5 57.9 %collective-permute-start.1 = (bf16[32,1536]{1,0:T(8,128)(2,1)S(1)}, bf16[32,1536]{1,0:T(8,128)(2,1)S(1)}, u32[]{:S(2)}, u32[]{:S(2)}) collective-permute-start(bf16[32,1536]{1,0:T(8,128)(2,1)S(1)} %get-tuple-element.707), channel_id=1, source_target_pairs={{0,7},{1,0},{2,1},{3,2},{4,3},{5,4},{6,5},{7,6},{8,15},{9,8},{10,9... | collective-permute-start | bytes 294920 | tf_op jit(solution)/shard_map/while/body/eval_jaxpr/ppermute | solution.py:91
  1630.8 57.7 %collective-permute-start.1 = (bf16[32,1536]{1,0:T(8,128)(2,1)S(1)}, bf16[32,1536]{1,0:T(8,128)(2,1)S(1)}, u32[]{:S(2)}, u32[]{:S(2)}) collective-permute-start(bf16[32,1536]{1,0:T(8,128)(2,1)S(1)} %get-tuple-element.707), channel_id=1, source_target_pairs={{0,7},{1,0},{2,1},{3,2},{4,3},{5,4},{6,5},{7,6},{8,15},{9,8},{10,9... | collective-permute-start | bytes 294920 | tf_op jit(solution)/shard_map/while/body/eval_jaxpr/ppermute | solution.py:91
  1727.0 57.7 %collective-permute-start.1 = (bf16[32,1536]{1,0:T(8,128)(2,1)S(1)}, bf16[32,1536]{1,0:T(8,128)(2,1)S(1)}, u32[]{:S(2)}, u32[]{:S(2)}) collective-permute-start(bf16[32,1536]{1,0:T(8,128)(2,1)S(1)} %get-tuple-element.707), channel_id=1, source_target_pairs={{0,7},{1,0},{2,1},{3,2},{4,3},{5,4},{6,5},{7,6},{8,15},{9,8},{10,9... | collective-permute-start | bytes 294920 | tf_op jit(solution)/shard_map/while/body/eval_jaxpr/ppermute | solution.py:91
  1823.2 60.1 %collective-permute-start.1 = (bf16[32,1536]{1,0:T(8,128)(2,1)S(1)}, bf16[32,1536]{1,0:T(8,128)(2,1)S(1)}, u32[]{:S(2)}, u32[]{:S(2)}) collective-permute-start(bf16[32,1536]{1,0:T(8,128)(2,1)S(1)} %get-tuple-element.707), channel_id=1, source_target_pairs={{0,7},{1,0},{2,1},{3,2},{4,3},{5,4},{6,5},{7,6},{8,15},{9,8},{10,9... | collective-permute-start | bytes 294920 | tf_op jit(solution)/shard_map/while/body/eval_jaxpr/ppermute | solution.py:91
  1884.2 818.7 %all-reduce.3.cloned.1.call-start = ((), (), s32[]{:S(2)}) async-start(), calls=%async_computation.4 | async-start | bytes 150994944 | tf_op jit(solution)/shard_map/psum | solution.py:101
  (41 other events, 948.5 us)
Sparse Core Ops, SparseCore 0:
  443.5 31.6 reduce-scatter.2
  1884.3 32.9 reduce-scatter.4
Sparse Core Ops, SparseCore 1:
  1889.4 813.4 all-reduce.2
where the time goes:
time: 2760 us
  matrix products  1550 us (56%)
  waiting for transfers between devices  897 us (32%)
  other arithmetic  143 us (5%)
  local copies, waits for them, and re-layouts  70.1 us (3%)
  loops' own time  41.4 us (2%)
    psum x1, waiting for transfers between devices, body(): dw1 = lax.psum(dw1, 'inner')  786 us
    dot_general x15, matrix products, _bwd(): dw1 = jnp.dot(h.T, dz, preferred_element_type=jnp.float32)  413 us
    dot_general x15, matrix products, _bwd(): dw2 = jnp.dot(a.T, dh, preferred_element_type=jnp.float32)  413 us
    dot_general x15, matrix products, _fwd(): u = jnp.dot(a, w2, preferred_element_type=jnp.float32)  237 us
    dot_general x15, matrix products, _bwd(): jnp.dot(dz, w1.T, preferred_element_type=jnp.float32)  189 us
    dot_general x15, matrix products, _bwd(): da = jnp.dot(dh, w2.T, preferred_element_type=jnp.float32)  180 us
    dot_general x15, matrix products, _bwd(): z = jnp.dot(h, w1, preferred_element_type=jnp.float32)  121 us
    ppermute x15, waiting for transfers between devices, fwd_tick(): inc = lax.ppermute(h, 'stage', fwd_perm)  78.2 us
  transfers between devices with their start and end apart: 33, of which 17 were waited for; matrix products, arithmetic and copies ran while one was open for 51% of the time, Pallas kernels for 0%

commit v1 on v0

v1 whole, which is shorter than its diff:
```python
import functools

import jax
import jax.numpy as jnp
from jax import lax
from jax.experimental import pallas as pl
from jax.experimental.pallas import tpu as pltpu
from jax.sharding import PartitionSpec as P

MESH = pl.DeviceIdType.MESH
BF, F32 = jnp.bfloat16, jnp.float32
NT = (((1,), (1,)), ((), ()))
C0 = 0.7978845608028654
C1 = 0.044715
VMEM_BYTES = 67043328


def gelu_parts(z):
    z2 = z * z
    t = jnp.tanh(z * (C0 + (C0 * C1) * z2))
    cdf = 0.5 + 0.5 * t
    return z * cdf, cdf + (0.5 * z) * (1.0 - t * t) * (C0 + (3.0 * C0 * C1) * z2)


def fb_kernel(x_ref, g_ref, w1_hbm, w2_hbm, y_ref, dx_ref, hall, gall,
              bufa, bufb, dg, act, hin, hout, gin, gout, tmp,
              wsem, tsem, xs, xr, gs, gr, fs, fr, bs, br, ys, yr, ds, dr, loc, ags, agr, *, ns):
    p = lax.axis_index("stage")
    q = lax.axis_index("inner")
    z, y = q // 4, q % 4
    d, f = bufa.shape
    ck = hin.shape[1]
    nmb = ns // 2
    sub = ck // nmb
    hf = ck // 2

    def at_stage(s):
        return {"data": 0, "inner": q, "stage": s}

    def at_plane(zz, yy):
        return {"data": 0, "inner": zz * 4 + yy, "stage": p}

    def rc(src, dst, ss, rs, dev):
        return pltpu.make_async_remote_copy(src_ref=src, dst_ref=dst, send_sem=ss, recv_sem=rs, device_id=dev, device_id_type=MESH)

    cw1 = pltpu.make_async_copy(w1_hbm, bufa, wsem.at[0])
    cw2 = pltpu.make_async_copy(w2_hbm, bufb, wsem.at[1])
    cw1.start()
    cw2.start()

    bar = pltpu.get_barrier_semaphore()
    for k in range(1, ns):
        pl.semaphore_signal(bar, inc=1, device_id=at_stage(lax.rem(p + k, ns)), device_id_type=MESH)
    for k in (1, 2, 3):
        pl.semaphore_signal(bar, inc=1, device_id=at_plane(lax.rem(z + k, 4), y), device_id_type=MESH)
        pl.semaphore_signal(bar, inc=1, device_id=at_plane(z, lax.rem(y + k, 4)), device_id_type=MESH)
    pl.semaphore_wait(bar, ns - 1 + 6)

    def mine(buf):
        return buf.at[p // nmb, pl.ds(pl.multiple_of(lax.rem(p, nmb) * sub, sub), sub)]

    def gather_x(s):
        return rc(x_ref, hin.at[s // nmb, pl.ds(pl.multiple_of(lax.rem(s, nmb) * sub, sub), sub)], xs, xr.at[s], at_stage(0))

    def gather_g(s):
        return rc(g_ref, gin.at[s // nmb, pl.ds(pl.multiple_of(lax.rem(s, nmb) * sub, sub), sub)], gs, gr.at[s], at_stage(ns - 1))

    @pl.when(p > 0)
    def _():
        gather_x(p).start()

    @pl.when(p < ns - 1)
    def _():
        gather_g(p).start()

    @pl.when(p == 0)
    def _():
        hin[0, :sub] = x_ref[...]

    @pl.when(p == ns - 1)
    def _():
        gin[1, ck - sub:] = g_ref[...]

    def hop_f(c):
        return rc(hout.at[c], hin.at[c], fs.at[c], fr.at[c], at_stage(lax.rem(p + 1, ns)))

    def hop_b(c):
        return rc(gout.at[c], gin.at[c], bs.at[c], br.at[c], at_stage(lax.rem(p + ns - 1, ns)))

    def put_y(c, m):
        return rc(hout.at[c, pl.ds(m * sub, sub)], y_ref, ys.at[c * nmb + m], yr, at_stage(c * nmb + m))

    def put_dx(c, m):
        return rc(gout.at[c, pl.ds(m * sub, sub)], dx_ref, ds.at[c * nmb + m], dr, at_stage(c * nmb + m))

    def blk(out, c, zz, yy):
        return out.at[zz, yy, c]

    def line(out, c, zz, yy):
        return out.at[:, yy, c] if c == 0 else out.at[zz, :, c]

    def half(ref, up, lead):
        rows = pl.ds(0, hf) if up else pl.ds(hf, hf)
        return ref.at[:, rows] if lead else ref.at[rows]

    def shift(c, first, k):
        along_z = (c == 0) == first
        return (lax.rem(z + k + 4, 4), y) if along_z else (z, lax.rem(y + k + 4, 4))

    def ag(buf, out, a, c, step, up):
        first = step in (0, 1)
        sgn = 1 if up else -1
        to = at_plane(*shift(c, first, sgn))
        j = (a * 2 + c) * 8 + step * 2 + (0 if up else 1)
        if step == 0:
            src, dst = buf.at[c], blk(out, c, z, y)
        elif step == 1:
            src = dst = half(blk(out, c, *shift(c, True, -sgn)), up, False)
        elif step == 2:
            src = dst = line(out, c, z, y)
        else:
            src = dst = half(line(out, c, *shift(c, False, -sgn)), up, True)
        return rc(src, dst, ags.at[j], agr.at[j], to)

    def own(buf, out, a, c):
        return pltpu.make_async_copy(buf.at[c], out.at[z, y, c], loc.at[a * 2 + c])

    def ag_start(buf, out, a, c, step):
        for up in (True, False):
            ag(buf, out, a, c, step, up).start()

    def ag_wait(buf, out, a, c, step):
        for up in (True, False):
            ag(buf, out, a, c, step, up).wait()

    H, G = (hin, hall, 0), (gin, gall, 1)

    def fwd(c):
        h = hin.at[c]
        rows = pl.ds(c * ck, ck)
        for j in range(0, f, 512):
            zz = jnp.dot(h[...], bufa[:, j:j + 512], preferred_element_type=F32)
            for r in range(0, ck, 32):
                a_, d_ = gelu_parts(zz[r:r + 32])
                act[r:r + 32, j:j + 512] = a_.astype(BF)
                dg[pl.ds(c * ck + r, 32), j:j + 512] = d_
        for j in range(0, d, 512):
            u = jnp.dot(act[...], bufb[:, j:j + 512], preferred_element_type=F32)
            hout[c, :, j:j + 512] = (h[:, j:j + 512].astype(F32) + u).astype(BF)

    def bwd(c):
        g = gin.at[c]
        for j in range(0, f, 512):
            da = jnp.dot(g[...], bufa[:, j:j + 512], preferred_element_type=F32)
            for r in range(0, ck, 32):
                act[r:r + 32, j:j + 512] = (da[r:r + 32] * dg[pl.ds(c * ck + r, 32), j:j + 512]).astype(BF)
        for j in range(0, d, 512):
            u = jnp.dot(act[...], bufb[:, j:j + 512], preferred_element_type=F32)
            gout[c, :, j:j + 512] = (g[:, j:j + 512].astype(F32) + u).astype(BF)

    cw1.wait()
    cw2.wait()
    for c in (0, 1):
        @pl.when(p == 0)
        def _():
            for m in range(nmb):
                if c or m:
                    gather_x(c * nmb + m).wait_recv()

        @pl.when(p > 0)
        def _():
            hop_f(c).wait_recv()

        own(*H, c).start()
        ag_start(*H, c, 0)
        if c == 1:
            own(*H, 0).wait()
            ag_wait(*H, 0, 0)
            ag_start(*H, 0, 1)
        fwd(c)

        @pl.when(p < ns - 1)
        def _():
            hop_f(c).start()

        @pl.when(p == ns - 1)
        def _():
            for m in range(nmb):
                if c * nmb + m < ns - 1:
                    put_y(c, m).start()
            if c == 1:
                pltpu.make_async_copy(hout.at[1, pl.ds(ck - sub, sub)], y_ref, yr).start()

    own(*H, 1).wait()
    ag_wait(*H, 1, 0)
    ag_start(*H, 1, 1)

    nt = 512
    def tload(i, s):
        return pltpu.make_async_copy(w1_hbm.at[:, pl.ds(pl.multiple_of(i * nt, nt), nt)], tmp.at[s], tsem.at[s])
    tload(0, 0).start()

    def t2(i, _):
        rows = pl.ds(pl.multiple_of(i * 128, 128), 128)
        bufa[:, rows] = bufb[rows, :].T
        return 0
    lax.fori_loop(0, f // 128, t2, 0)

    def t1(i, _):
        s = lax.rem(i, 2)

        @pl.when(i + 1 < f // nt)
        def _():
            tload(i + 1, 1 - s).start()
        tload(i, s).wait()
        for r in range(0, nt, 128):
            bufb[pl.ds(pl.multiple_of(i * nt + r, 128), 128), :] = tmp[s, :, r:r + 128].T
        return 0
    lax.fori_loop(0, f // nt, t1, 0)

    def ag_rest():
        for c in (0, 1):
            ag_wait(*H, c, 1)
            ag_start(*H, c, 2)
        for c in (0, 1):
            ag_wait(*H, c, 2)
            ag_start(*H, c, 3)

    @pl.when(p < ns - 2)
    def _():
        ag_rest()

    for c in (0, 1):
        @pl.when(p == ns - 1)
        def _():
            for m in range(nmb):
                if c * nmb + m < ns - 1:
                    gather_g(c * nmb + m).wait_recv()

        @pl.when(p < ns - 1)
        def _():
            hop_b(c).wait_recv()

        own(*G, c).start()
        ag_start(*G, c, 0)
        if c == 1:
            own(*G, 0).wait()
            ag_wait(*G, 0, 0)
            ag_start(*G, 0, 1)
        bwd(c)

        @pl.when(p > 0)
        def _():
            hop_b(c).start()

        @pl.when(p == 0)
        def _():
            for m in range(nmb):
                if c * nmb + m > 0:
                    put_dx(c, m).start()
            if c == 0:
                pltpu.make_async_copy(gout.at[0, pl.ds(0, sub)], dx_ref, dr).start()

    own(*G, 1).wait()
    ag_wait(*G, 1, 0)
    ag_start(*G, 1, 1)

    @pl.when(p >= ns - 2)
    def _():
        ag_rest()
    for c in (0, 1):
        ag_wait(*G, c, 1)
        ag_start(*G, c, 2)
    for c in (0, 1):
        ag_wait(*G, c, 2)
        ag_start(*G, c, 3)

    @pl.when(p > 0)
    def _():
        gather_x(p).wait_send()
        hop_b(0).wait_send()
        hop_b(1).wait_send()
        put_dx(0, 0).wait_recv()

    @pl.when(p == 0)
    def _():
        for s in range(1, ns):
            put_dx(s // nmb, s % nmb).wait_send()
        pltpu.make_async_copy(gout.at[0, pl.ds(0, sub)], dx_ref, dr).wait()

    @pl.when(p < ns - 1)
    def _():
        gather_g(p).wait_send()
        hop_f(0).wait_send()
        hop_f(1).wait_send()
        put_y(0, 0).wait_recv()

    @pl.when(p == ns - 1)
    def _():
        for s in range(ns - 1):
            put_y(s // nmb, s % nmb).wait_send()
        pltpu.make_async_copy(hout.at[1, pl.ds(ck - sub, sub)], y_ref, yr).wait()

    for c in (0, 1):
        ag_wait(*H, c, 3)
        ag_wait(*G, c, 3)


def fb(x, g, w1, w2, ns=8, ni=16):
    b, d = x.shape
    f = w1.shape[1]
    ck = b * ns // 2
    dma = pltpu.SemaphoreType.DMA
    vm = pl.BlockSpec(memory_space=pltpu.VMEM)
    hbm = pl.BlockSpec(memory_space=pl.ANY)
    allt = jax.ShapeDtypeStruct((4, 4, 2, ck, d), BF)
    y, dx, h, gg = pl.pallas_call(
        functools.partial(fb_kernel, ns=ns),
        in_specs=[vm, vm, hbm, hbm],
        out_specs=[hbm] * 4,
        out_shape=[jax.ShapeDtypeStruct((b, d), BF)] * 2 + [allt] * 2,
        scratch_shapes=[
            pltpu.VMEM((d, f), BF), pltpu.VMEM((f, d), BF), pltpu.VMEM((2 * ck, f), F32), pltpu.VMEM((ck, f), BF),
            pltpu.VMEM((2, ck, d), BF), pltpu.VMEM((2, ck, d), BF), pltpu.VMEM((2, ck, d), BF), pltpu.VMEM((2, ck, d), BF),
            pltpu.VMEM((2, d, 512), BF),
            dma((2,)), dma((2,)), dma, dma((ns,)), dma, dma((ns,)), dma((2,)), dma((2,)), dma((2,)), dma((2,)),
            dma((ns,)), dma, dma((ns,)), dma, dma((4,)), dma((32,)), dma((32,)),
        ],
        compiler_params=pltpu.CompilerParams(vmem_limit_bytes=VMEM_BYTES, collective_id=0, has_side_effects=True),
        name="fb",
    )(x, g, w1, w2)
    return y, dx, h.reshape(-1, d), gg.reshape(-1, d)


def wgrad_kernel(w1_ref, w2_ref, h_ref, g_ref, dw1_ref, dw2_ref, w1t, at, dzt, z0, z1, d0, d1, *, tc):
    t, d = h_ref.shape
    f = w2_ref.shape[0]
    n = t // tc
    zs, ds = (z0, z1), (d0, d1)
    for r in range(0, f, 128):
        w1t[r:r + 128, :] = w1_ref[:, r:r + 128].T

    def dots(i):
        rows = pl.ds(i * tc, tc)
        zs[i % 2][...] = lax.dot_general(w1t[...], h_ref[rows, :], NT, preferred_element_type=F32)
        ds[i % 2][...] = lax.dot_general(w2_ref[...], g_ref[rows, :], NT, preferred_element_type=F32)

    def elem(i):
        cols = pl.ds(i * tc, tc)
        for r in range(0, f, 32):
            a, da = gelu_parts(zs[i % 2][r:r + 32, :])
            at[r:r + 32, cols] = a.astype(BF)
            dzt[r:r + 32, cols] = (ds[i % 2][r:r + 32, :] * da).astype(BF)

    dots(0)
    for i in range(1, n):
        dots(i)
        elem(i - 1)
    elem(n - 1)

    for j in range(0, d, 512):
        cols = pl.ds(j, 512)
        p1 = jnp.dot(dzt[...], h_ref[:, cols], preferred_element_type=F32)
        for r in range(0, 512, 128):
            dw1_ref[pl.ds(j + r, 128), :] = p1[:, r:r + 128].T
        dw2_ref[:, cols] = jnp.dot(at[...], g_ref[:, cols], preferred_element_type=F32)


def wgrad(w1, w2, h, g, f=512, tc=512):
    d, ff = w1.shape
    t = h.shape[0]
    nb = ff // f
    once = pl.Buffered(1)
    return pl.pallas_call(
        functools.partial(wgrad_kernel, tc=tc),
        grid=(nb,),
        in_specs=[
            pl.BlockSpec((d, f), lambda i: (0, i)),
            pl.BlockSpec((f, d), lambda i: (i, 0)),
            pl.BlockSpec((t, d), lambda i: (0, 0), pipeline_mode=once),
            pl.BlockSpec((t, d), lambda i: (0, 0), pipeline_mode=once),
        ],
        out_specs=[pl.BlockSpec((d, f), lambda i: (0, i)), pl.BlockSpec((f, d), lambda i: (i, 0))],
        out_shape=[jax.ShapeDtypeStruct((d, ff), F32), jax.ShapeDtypeStruct((ff, d), F32)],
        scratch_shapes=[pltpu.VMEM((f, d), BF), pltpu.VMEM((f, t), BF), pltpu.VMEM((f, t), BF)] + [pltpu.VMEM((f, tc), F32)] * 4,
        compiler_params=pltpu.CompilerParams(vmem_limit_bytes=VMEM_BYTES, dimension_semantics=("arbitrary",)),
        cost_estimate=pl.CostEstimate(flops=8 * t * d * ff, bytes_accessed=12 * d * ff + 4 * t * d, transcendentals=t * ff),
        name="wgrad",
    )(w1, w2, h, g)


def solution(mesh):
    def body(x, g, w1, w2):
        w1, w2 = w1[0, 0], w2[0, 0]
        y, dx, h, gg = fb(x[0], g[0], w1, w2)
        dw1, dw2 = wgrad(w1, w2, h, gg)
        return y[None], dx[None], dw1[None, None], dw2[None, None]

    tok = P(("data", "stage"), "inner", None)
    wsp = P(None, "stage", None, None)
    dsp = P("data", "stage", None, None)
    return jax.shard_map(body, mesh=mesh, in_specs=(tok, tok, wsp, wsp), out_specs=(tok, tok, dsp, dsp), check_vma=False)
```

time: 2760 us -> 607 us (0.22)
  matrix products: 1550 us -> 0 us
  waiting for transfers between devices: 897 us -> 0 us
  Pallas kernels: 0 us -> 600 us
  other arithmetic: 143 us -> 0 us
  local copies, waits for them, and re-layouts: 70.1 us -> 3.08 us
  loops' own time: 41.4 us -> 0 us
    dot_general x90 -> x0, matrix products: 1550 us -> none  [the longest x15 413 us: _bwd(): dw1 = jnp.dot(h.T, dz, preferred_element_type=jnp.float32)]
    psum x1 -> x0, waiting for transfers between devices: 786 us -> none  [body(): dw1 = lax.psum(dw1, 'inner')]
    pallas_call x0 -> x2, Pallas kernels: none -> 600 us  [the longest x1 341 us: wgrad(): pl.pallas_call(functools.partial(wgrad_kernel, tc=tc), grid=(nb,), in_spe...]
    ppermute x30 -> x0, waiting for transfers between devices: 78.3 us -> none  [the longest x15 78.2 us: fwd_tick(): inc = lax.ppermute(h, 'stage', fwd_perm)]
    another operation x60 -> x0, other arithmetic: 74.1 us -> none
    scatter x45 -> x0, other arithmetic: 52.7 us -> none  [the longest x15 22.6 us: fwd_tick(): saved = saved.at[v, mi].set(jnp.where(ok, jnp.stack(hs), saved[v, mi]))]
    unnamed x6 -> x2, local copies, waits for them, and re-layouts: 48.8 us -> 3.08 us
    another operation x2 -> x0, loops' own time: 41.4 us -> none  [the longest x1 20.7 us: body(): lax.scan(fwd_tick, (act0, per_mb0, saved0, per_mb0), ticks)]
  transfers between devices with their start and end apart: 33 -> 0, of which waited for: 17 -> 0; matrix products, arithmetic and copies ran while one was open for 51% -> 0% of each run, Pallas kernels for 0% -> 0%
where the time goes in v1:
time: 607 us; the launch traced here: 604 us
  Pallas kernels  600 us (99%)
    pallas_call x1, Pallas kernels, wgrad(): pl.pallas_call(functools.partial(wgrad_kernel, tc=tc), grid=(nb,), in_spe...  341 us
    pallas_call x1, Pallas kernels, fb(): pl.pallas_call(functools.partial(fb_kernel, ns=ns), in_specs=[vm, vm, hbm...  259 us

profile of v1, /device:TPU:0, one launch (start us, length us, event | category | flops | bytes accessed | tf_op | source)
XLA Modules:
  0.0 603.8 jit_solution(9535364681119161966)
XLA Ops:
  0.6 259.2 %fb.1 = (bf16[32,1536]{1,0:T(8,128)(2,1)}, bf16[32,1536]{1,0:T(8,128)(2,1)}, bf16[4,4,2,128,1536]{4,3,2,1,0:T(8,128)(2,1)}, bf16[4,4,2,128,1536]{4,3,2,1,0:T(8,128)(2,1)}) custom-call(bf16[32,1536]{1,0:T(8,128)(2,1)} %bitcast.14, bf16[32,1536]{1,0:T(8,128)(2,1)} %bitcast.15, bf16[1536,6144]{1,0:T(8,128)(2,1)} %bitcast.10, bf16[6144,1536]{1,0:T(8,128)(2,1)} %bitcast.12), custom_call_target="tpu_custom_call" | custom-call | tf_op jit(solution)/shard_map/fb/pallas_call | solution.py:317
  259.9 340.7 %wgrad.1 = (f32[1536,6144]{1,0:T(8,128)}, f32[6144,1536]{1,0:T(8,128)}) custom-call(bf16[1536,6144]{1,0:T(8,128)(2,1)} %bitcast.11, bf16[6144,1536]{1,0:T(8,128)(2,1)} %bitcast.13, bf16[4096,1536]{1,0:T(8,128)(2,1)} %bitcast.18, bf16[4096,1536]{1,0:T(8,128)(2,1)} %bitcast.19), custom_call_target="tpu_custom_call" | custom-call | flops 309237645312 | bytes 138412032 | tf_op jit(solution)/shard_map/wgrad/pallas_call | solution.py:374
  600.6 1.5 copy.10
  602.1 1.5 copy.11

commit v2 on v1

v2 whole, which is shorter than its diff:
```python
import functools

import jax
import jax.numpy as jnp
from jax import lax
from jax.experimental import pallas as pl
from jax.experimental.pallas import tpu as pltpu
from jax.sharding import PartitionSpec as P

MESH = pl.DeviceIdType.MESH
BF, F32 = jnp.bfloat16, jnp.float32
NT = (((1,), (1,)), ((), ()))
C0 = 0.7978845608028654
C1 = 0.044715
VMEM_BYTES = 67043328
PRE = 3
NB = 9


def gelu_parts(z):
    z2 = z * z
    t = jnp.tanh(z * (C0 + (C0 * C1) * z2))
    cdf = 0.5 + 0.5 * t
    return z * cdf, cdf + (0.5 * z) * (1.0 - t * t) * (C0 + (3.0 * C0 * C1) * z2)


def fb_kernel(x_ref, g_ref, w1_hbm, w2_hbm, y_ref, dx_ref, hall, gall, zall,
              bufa, bufb, dg, act, hin, hout, gin, gout, tmp, hbuf, zb0, zb1, zb2,
              wsem, tsem, hsem, zsem, xs, xr, gs, gr, fs, fr, bs, br, ys, yr, ds, dr, loc, ags, agr, *, ns):
    p = lax.axis_index("stage")
    q = lax.axis_index("inner")
    z, y = q // 4, q % 4
    d, f = bufa.shape
    ck = hin.shape[1]
    nmb = ns // 2
    sub = ck // nmb
    hf = ck // 2

    def at_stage(s):
        return {"data": 0, "inner": q, "stage": s}

    def at_plane(zz, yy):
        return {"data": 0, "inner": zz * 4 + yy, "stage": p}

    def rc(src, dst, ss, rs, dev):
        return pltpu.make_async_remote_copy(src_ref=src, dst_ref=dst, send_sem=ss, recv_sem=rs, device_id=dev, device_id_type=MESH)

    cw1 = pltpu.make_async_copy(w1_hbm, bufa, wsem.at[0])
    cw2 = pltpu.make_async_copy(w2_hbm, bufb, wsem.at[1])
    cw1.start()
    cw2.start()

    bar = pltpu.get_barrier_semaphore()
    for k in range(1, ns):
        pl.semaphore_signal(bar, inc=1, device_id=at_stage(lax.rem(p + k, ns)), device_id_type=MESH)
    for k in (1, 2, 3):
        pl.semaphore_signal(bar, inc=1, device_id=at_plane(lax.rem(z + k, 4), y), device_id_type=MESH)
        pl.semaphore_signal(bar, inc=1, device_id=at_plane(z, lax.rem(y + k, 4)), device_id_type=MESH)
    pl.semaphore_wait(bar, ns - 1 + 6)

    def mine(buf):
        return buf.at[p // nmb, pl.ds(pl.multiple_of(lax.rem(p, nmb) * sub, sub), sub)]

    def gather_x(s):
        return rc(x_ref, hin.at[s // nmb, pl.ds(pl.multiple_of(lax.rem(s, nmb) * sub, sub), sub)], xs, xr.at[s], at_stage(0))

    def gather_g(s):
        return rc(g_ref, gin.at[s // nmb, pl.ds(pl.multiple_of(lax.rem(s, nmb) * sub, sub), sub)], gs, gr.at[s], at_stage(ns - 1))

    @pl.when(p > 0)
    def _():
        gather_x(p).start()

    @pl.when(p < ns - 1)
    def _():
        gather_g(p).start()

    @pl.when(p == 0)
    def _():
        hin[0, :sub] = x_ref[...]

    @pl.when(p == ns - 1)
    def _():
        gin[1, ck - sub:] = g_ref[...]

    def hop_f(c):
        return rc(hout.at[c], hin.at[c], fs.at[c], fr.at[c], at_stage(lax.rem(p + 1, ns)))

    def hop_b(c):
        return rc(gout.at[c], gin.at[c], bs.at[c], br.at[c], at_stage(lax.rem(p + ns - 1, ns)))

    def put_y(c, m):
        return rc(hout.at[c, pl.ds(m * sub, sub)], y_ref, ys.at[c * nmb + m], yr, at_stage(c * nmb + m))

    def put_dx(c, m):
        return rc(gout.at[c, pl.ds(m * sub, sub)], dx_ref, ds.at[c * nmb + m], dr, at_stage(c * nmb + m))

    def blk(out, c, zz, yy):
        return out.at[zz, yy, c]

    def line(out, c, zz, yy):
        return out.at[:, yy, c] if c == 0 else out.at[zz, :, c]

    def half(ref, up, lead):
        rows = pl.ds(0, hf) if up else pl.ds(hf, hf)
        return ref.at[:, rows] if lead else ref.at[rows]

    def shift(c, first, k):
        along_z = (c == 0) == first
        return (lax.rem(z + k + 4, 4), y) if along_z else (z, lax.rem(y + k + 4, 4))

    def ag(buf, out, a, c, step, up):
        first = step in (0, 1)
        sgn = 1 if up else -1
        to = at_plane(*shift(c, first, sgn))
        j = (a * 2 + c) * 8 + step * 2 + (0 if up else 1)
        if step == 0:
            src, dst = buf.at[c], blk(out, c, z, y)
        elif step == 1:
            src = dst = half(blk(out, c, *shift(c, True, -sgn)), up, False)
        elif step == 2:
            src = dst = line(out, c, z, y)
        else:
            src = dst = half(line(out, c, *shift(c, False, -sgn)), up, True)
        return rc(src, dst, ags.at[j], agr.at[j], to)

    def own(buf, out, a, c):
        return pltpu.make_async_copy(buf.at[c], out.at[z, y, c], loc.at[a * 2 + c])

    def ag_start(buf, out, a, c, step):
        for up in (True, False):
            ag(buf, out, a, c, step, up).start()

    def ag_wait(buf, out, a, c, step):
        for up in (True, False):
            ag(buf, out, a, c, step, up).wait()

    H, G = (hin, hall, 0), (gin, gall, 1)
    last = ns - 1

    def ag_go(who, step):
        for c in (0, 1):
            ag_wait(*who, c, step - 1)
            ag_start(*who, c, step)

    def ag_end(who):
        for c in (0, 1):
            ag_wait(*who, c, 3)

    def ag_in(who, c):
        for cc in (0, 1):
            @pl.when(c == cc)
            def _():
                own(*who, cc).start()
                ag_start(*who, cc, 0)

    def ag_in_end(who):
        for c in (0, 1):
            own(*who, c).wait()
        ag_go(who, 1)

    def up(c, src, k):
        for j in range(0, d, 512):
            u = jnp.dot(act[k], bufb[:, j:j + 512], preferred_element_type=F32)
            hout[c, :, j:j + 512] = (src[:, j:j + 512].astype(F32) + u).astype(BF)

    def rows_of(c, r, n):
        return pl.ds(pl.multiple_of(c * ck + r, n), n)

    def fwd(c):
        h = hin.at[c]
        for j in range(0, f, 512):
            zz = jnp.dot(h[...], bufa[:, j:j + 512], preferred_element_type=F32)
            for r in range(0, ck, 32):
                a_, d_ = gelu_parts(zz[r:r + 32])
                act[0, r:r + 32, j:j + 512] = a_.astype(BF)
                dg[rows_of(c, r, 32), j:j + 512] = d_

        @pl.when(c == 0)
        def _():
            cw2.wait()
        up(c, h, 0)

    def bwd(c):
        g = gin.at[c]
        for j in range(0, f, 512):
            da = jnp.dot(g[...], bufa[:, j:j + 512], preferred_element_type=F32)
            for r in range(0, ck, 32):
                act[0, r:r + 32, j:j + 512] = (da[r:r + 32] * dg[rows_of(c, r, 32), j:j + 512]).astype(BF)
        for j in range(0, d, 512):
            u = jnp.dot(act[0], bufb[:, j:j + 512], preferred_element_type=F32)
            gout[c, :, j:j + 512] = (g[:, j:j + 512].astype(F32) + u).astype(BF)

    def turn(c):
        h, g = hin.at[c], gin.at[c]
        for j in range(0, f, 512):
            zz = jnp.dot(h[...], bufa[:, j:j + 512], preferred_element_type=F32)
            for r in range(0, ck, 32):
                a_, d_ = gelu_parts(zz[r:r + 32])
                act[c, r:r + 32, j:j + 512] = a_.astype(BF)
                act[2, r:r + 32, j:j + 512] = (dg[rows_of(c, r, 32), j:j + 512] * d_).astype(BF)
        for j in range(0, d, 512):
            u = lax.dot_general(act[2], bufa[j:j + 512, :], NT, preferred_element_type=F32)
            gout[c, :, j:j + 512] = (g[:, j:j + 512].astype(F32) + u).astype(BF)

    cw1.wait()

    @pl.when(p < last)
    def _():
        @pl.loop(0, 2)
        def _(c):
            @pl.when(p == 0)
            def _():
                for m in range(nmb):
                    @pl.when(c * nmb + m > 0)
                    def _():
                        gather_x(c * nmb + m).wait_recv()

            @pl.when(p > 0)
            def _():
                hop_f(c).wait_recv()
            ag_in(H, c)
            fwd(c)
            hop_f(c).start()
        ag_in_end(H)

    @pl.when(p == last)
    def _():
        cw2.wait()
        for s in range(last):
            gather_g(s).wait_recv()
        for c in (0, 1):
            own(*G, c).start()
            ag_start(*G, c, 0)

        @pl.loop(0, 2)
        def _(c):
            for j in range(0, f, 512):
                dg[rows_of(c, 0, ck), j:j + 512] = lax.dot_general(gin[c], bufb[j:j + 512, :], NT, preferred_element_type=F32)
        for c in (0, 1):
            own(*G, c).wait()
        for step in (1, 2, 3):
            ag_go(G, step)

        @pl.loop(0, 2)
        def _(c):
            hop_f(c).wait_recv()
            ag_in(H, c)
            turn(c)
            hop_b(c).start()

        @pl.loop(0, 2)
        def _(c):
            up(c, hin.at[c], c)
            for m in range(nmb):
                @pl.when(c * nmb + m < last)
                def _():
                    put_y(c, m).start()
        pltpu.make_async_copy(hout.at[1, pl.ds(ck - sub, sub)], y_ref, yr).start()
        ag_in_end(H)
        ag_go(H, 2)

    @pl.when(p < last - 1)
    def _():
        ag_go(H, 2)

    nt = 512

    def tload(i, s):
        return pltpu.make_async_copy(w1_hbm.at[:, pl.ds(pl.multiple_of(i * nt, nt), nt)], tmp.at[s], tsem.at[s])
    tload(0, 0).start()

    @pl.loop(0, f // nt)
    def _(i):
        for r in range(0, nt, 128):
            rows = pl.ds(pl.multiple_of(i * nt + r, 128), 128)
            bufa[:, rows] = bufb[rows, :].T

    @pl.loop(0, f // nt)
    def _(i):
        s = lax.rem(i, 2)

        @pl.when(i + 1 < f // nt)
        def _():
            tload(i + 1, 1 - s).start()
        tload(i, s).wait()
        for r in range(0, nt, 128):
            bufb[pl.ds(pl.multiple_of(i * nt + r, 128), 128), :] = tmp[s, :, r:r + 128].T

    @pl.when(p == last - 1)
    def _():
        ag_go(H, 2)

    nf = zall.shape[0] // 512
    nt_z = zall.shape[1] // 512
    zb = (zb0, zb1, zb2)

    def hload(t):
        s = lax.rem(t, 2)
        return pltpu.make_async_copy(hall.at[t // 2, pl.ds(2 * s, 2)], hbuf.at[s], hsem.at[s])

    def zput(n, u):
        rows = pl.ds(pl.multiple_of(lax.rem(n, nf) * 512, 512), 512)
        cols = pl.ds(pl.multiple_of((n // nf) * 512, 512), 512)
        return pltpu.make_async_copy(zb[u], zall.at[rows, cols], zsem.at[u])

    def zwork(t0, t1):
        hload(t0).start()

        @pl.loop(t0, t1)
        def _(t):
            hload(t).wait()

            @pl.when(t + 1 < t1)
            def _():
                hload(t + 1).start()

            @pl.loop(0, nf // 3)
            def _(k):
                for u in range(3):
                    n = t * nf + 3 * k + u

                    @pl.when(n >= t0 * nf + 3)
                    def _():
                        zput(n - 3, u).wait()
                    rows = pl.ds(pl.multiple_of((3 * k + u) * 512, 512), 512)
                    hc = hbuf[lax.rem(t, 2)].reshape(512, d)
                    zb[u][...] = lax.dot_general(bufb[rows, :], hc, NT, preferred_element_type=F32)
                    zput(n, u).start()
        for u in range(3):
            zput(t1 * nf - 3 + u, u).wait()

    pre = jnp.where(p < 2, PRE, 0)
    mid = jnp.where(p < 2, (nt_z + PRE) // 2, nt_z // 2)

    @pl.when(p < 4)
    def _():
        ag_go(H, 3)

    @pl.when(p < 2)
    def _():
        ag_end(H)
        zwork(0, pre)

    @pl.when(p < last)
    def _():
        @pl.loop(0, 2)
        def _(c):
            hop_b(c).wait_recv()
            ag_in(G, c)
            bwd(c)

            @pl.when(p > 0)
            def _():
                hop_b(c).start()

            @pl.when(p == 0)
            def _():
                for m in range(nmb):
                    @pl.when(c * nmb + m > 0)
                    def _():
                        put_dx(c, m).start()

        @pl.when(p == 0)
        def _():
            pltpu.make_async_copy(gout.at[0, pl.ds(0, sub)], dx_ref, dr).start()
        ag_in_end(G)

    @pl.when(p >= 4)
    def _():
        ag_go(H, 3)

    @pl.when(p >= 2)
    def _():
        ag_end(H)

    @pl.when(p < last)
    def _():
        ag_go(G, 2)
    zwork(pre, mid)

    @pl.when(p < last)
    def _():
        ag_go(G, 3)
    zwork(mid, nt_z)
    ag_end(G)

    @pl.when(p > 0)
    def _():
        gather_x(p).wait_send()
        hop_b(0).wait_send()
        hop_b(1).wait_send()
        put_dx(0, 0).wait_recv()

    @pl.when(p == 0)
    def _():
        for s in range(1, ns):
            put_dx(s // nmb, s % nmb).wait_send()
        pltpu.make_async_copy(gout.at[0, pl.ds(0, sub)], dx_ref, dr).wait()

    @pl.when(p < ns - 1)
    def _():
        gather_g(p).wait_send()
        hop_f(0).wait_send()
        hop_f(1).wait_send()
        put_y(0, 0).wait_recv()

    @pl.when(p == ns - 1)
    def _():
        for s in range(ns - 1):
            put_y(s // nmb, s % nmb).wait_send()
        pltpu.make_async_copy(hout.at[1, pl.ds(ck - sub, sub)], y_ref, yr).wait()


def fb(x, g, w1, w2, nz, ns=8):
    b, d = x.shape
    f = w1.shape[1]
    ck = b * ns // 2
    dma = pltpu.SemaphoreType.DMA
    vm = pl.BlockSpec(memory_space=pltpu.VMEM)
    hbm = pl.BlockSpec(memory_space=pl.ANY)
    allt = jax.ShapeDtypeStruct((4, 4, 2, ck, d), BF)
    y, dx, h, gg, z = pl.pallas_call(
        functools.partial(fb_kernel, ns=ns),
        in_specs=[vm, vm, hbm, hbm],
        out_specs=[hbm] * 5,
        out_shape=[jax.ShapeDtypeStruct((b, d), BF)] * 2 + [allt] * 2 + [jax.ShapeDtypeStruct((nz, 32 * ck), F32)],
        scratch_shapes=[
            pltpu.VMEM((d, f), BF), pltpu.VMEM((f, d), BF), pltpu.VMEM((2 * ck, f), F32), pltpu.VMEM((3, ck, f), BF),
            pltpu.VMEM((2, ck, d), BF), pltpu.VMEM((2, ck, d), BF), pltpu.VMEM((2, ck, d), BF), pltpu.VMEM((2, ck, d), BF),
            pltpu.VMEM((2, d, 512), BF), pltpu.VMEM((2, 2, 2, ck, d), BF), pltpu.VMEM((512, 512), F32), pltpu.VMEM((512, 512), F32), pltpu.VMEM((512, 512), F32),
            dma((2,)), dma((2,)), dma((2,)), dma((3,)), dma, dma((ns,)), dma, dma((ns,)), dma((2,)), dma((2,)), dma((2,)), dma((2,)),
            dma((ns,)), dma, dma((ns,)), dma, dma((4,)), dma((32,)), dma((32,)),
        ],
        compiler_params=pltpu.CompilerParams(vmem_limit_bytes=VMEM_BYTES, collective_id=0, has_side_effects=True),
        name="fb",
    )(x, g, w1, w2)
    return y, dx, h.reshape(-1, d), gg.reshape(-1, d), z


def wgrad_kernel(z_hbm, w2_ref, h_hbm, g_hbm, dw1_ref, dw2_ref, h_ref, g_ref, at, dzt, z0, z1, d0, d1, hsem, zsem):
    b = pl.program_id(0)
    nb = pl.num_programs(0)
    t, d = h_ref.shape
    f = w2_ref.shape[0]
    tc = d0.shape[1]
    n = t // tc
    half = t // 2
    zs, ds = (z0, z1), (d0, d1)

    def zget(blk, i):
        rows = pl.ds(pl.multiple_of(blk * f, f), f)
        return pltpu.make_async_copy(z_hbm.at[rows, pl.ds(i * half, half)], zs[i], zsem.at[i])

    gget = pltpu.make_async_copy(g_hbm, g_ref, hsem.at[0])
    hget = pltpu.make_async_copy(h_hbm, h_ref, hsem.at[1])

    @pl.when(b == 0)
    def _():
        gget.start()
        zget(0, 0).start()
        zget(0, 1).start()
        hget.start()
        gget.wait()

    def dots(i):
        rows = pl.ds(i * tc, tc)
        ds[i % 2][...] = lax.dot_general(w2_ref[...], g_ref[rows, :], NT, preferred_element_type=F32)

    def elem(i):
        cols = pl.ds(i * tc, tc)
        off = (i * tc) % half
        for r in range(0, f, 32):
            a, da = gelu_parts(zs[i * tc // half][r:r + 32, off:off + tc])
            at[r:r + 32, cols] = a.astype(BF)
            dzt[r:r + 32, cols] = (ds[i % 2][r:r + 32, :] * da).astype(BF)

    zget(b, 0).wait()
    dots(0)
    for i in range(1, n // 2 + 1):
        dots(i)
        elem(i - 1)
    zget(b, 1).wait()

    @pl.when(b + 1 < nb)
    def _():
        zget(b + 1, 0).start()

    @pl.when(b == 0)
    def _():
        hget.wait()
    for i in range(n // 2 + 1, n):
        dots(i)
        elem(i - 1)
    elem(n - 1)
    for j in range(0, d, 512):
        cols = pl.ds(j, 512)
        p1 = jnp.dot(dzt[...], h_ref[:, cols], preferred_element_type=F32)
        for r in range(0, 512, 128):
            dw1_ref[pl.ds(j + r, 128), :] = p1[:, r:r + 128].T
        dw2_ref[:, cols] = jnp.dot(at[...], g_ref[:, cols], preferred_element_type=F32)

    @pl.when(b + 1 < nb)
    def _():
        zget(b + 1, 1).start()


def wgrad(z, w2, h, g, f=512, tc=512):
    ff, d = w2.shape
    t = h.shape[0]
    nb = z.shape[0] // f
    hbm = pl.BlockSpec(memory_space=pl.ANY)
    dma = pltpu.SemaphoreType.DMA
    return pl.pallas_call(
        wgrad_kernel,
        grid=(nb,),
        in_specs=[hbm, pl.BlockSpec((f, d), lambda i: (i, 0)), hbm, hbm],
        out_specs=[pl.BlockSpec((d, f), lambda i: (0, i)), pl.BlockSpec((f, d), lambda i: (i, 0))],
        out_shape=[jax.ShapeDtypeStruct((d, ff), F32), jax.ShapeDtypeStruct((ff, d), F32)],
        scratch_shapes=[pltpu.VMEM((t, d), BF)] * 2 + [pltpu.VMEM((f, t), BF)] * 2 + [pltpu.VMEM((f, t // 2), F32)] * 2 + [pltpu.VMEM((f, tc), F32)] * 2
        + [dma((2,)), dma((2,))],
        compiler_params=pltpu.CompilerParams(vmem_limit_bytes=VMEM_BYTES, dimension_semantics=("arbitrary",)),
        cost_estimate=pl.CostEstimate(flops=6 * t * d * ff, bytes_accessed=10 * d * ff + 4 * t * d + 4 * t * ff, transcendentals=t * ff),
        name="wgrad",
    )(z, w2, h, g)


def share_kernel(w1t, w2, h_hbm, g_hbm, s1, s2, h_ref, g_ref, at, dzt, hsem, gsem, *, tc):
    t = h_ref.shape[0]
    n = t // tc

    def part(src, dst, sem, i):
        rows = pl.ds(i * tc if isinstance(i, int) else pl.multiple_of(i * tc, tc), tc)
        return pltpu.make_async_copy(src.at[rows], dst.at[rows], sem.at[i])
    for i in range(n):
        part(h_hbm, h_ref, hsem, i).start()
        part(g_hbm, g_ref, gsem, i).start()

    @pl.loop(0, n)
    def _(i):
        rows = pl.ds(pl.multiple_of(i * tc, tc), tc)
        part(h_hbm, h_ref, hsem, i).wait()
        part(g_hbm, g_ref, gsem, i).wait()
        z = lax.dot_general(w1t[...], h_ref[rows, :], NT, preferred_element_type=F32)
        da = lax.dot_general(w2[...], g_ref[rows, :], NT, preferred_element_type=F32)
        a, dg = gelu_parts(z)
        at[:, rows] = a.astype(BF)
        dzt[:, rows] = (da * dg).astype(BF)

    @pl.loop(0, h_ref.shape[1] // 512)
    def _(j):
        cols = pl.ds(pl.multiple_of(j * 512, 512), 512)
        s1[:, cols] = jnp.dot(dzt[...], h_ref[:, cols], preferred_element_type=F32)
        s2[:, cols] = jnp.dot(at[...], g_ref[:, cols], preferred_element_type=F32)


def share(w1t, w2, h, g, tc=1024):
    fs, d = w2.shape
    t = h.shape[0]
    vm = pl.BlockSpec(memory_space=pltpu.VMEM)
    hbm = pl.BlockSpec(memory_space=pl.ANY)
    dma = pltpu.SemaphoreType.DMA
    return pl.pallas_call(
        functools.partial(share_kernel, tc=tc),
        in_specs=[vm, vm, hbm, hbm],
        out_specs=[vm, vm],
        out_shape=[jax.ShapeDtypeStruct((fs, d), F32)] * 2,
        scratch_shapes=[pltpu.VMEM((t, d), BF)] * 2 + [pltpu.VMEM((fs, t), BF)] * 2 + [dma((t // tc,)), dma((t // tc,))],
        compiler_params=pltpu.CompilerParams(vmem_limit_bytes=VMEM_BYTES),
        cost_estimate=pl.CostEstimate(flops=16 * t * d * fs, bytes_accessed=4 * t * d, transcendentals=t * fs),
        name="share",
    )(w1t, w2, h, g)


def finish_kernel(s1, s2, dw1_in, dw2_in, dw1, dw2):
    del dw1_in, dw2_in
    for r in range(0, s1.shape[1], 256):
        dw1[pl.ds(r, 256), :] = s1[:, r:r + 256].T
    dw2[...] = s2[...]


def finish(s1, s2, dw1, dw2, first, f=512):
    n, d = s1.shape
    hbm = pl.BlockSpec(memory_space=pl.ANY)
    row = pl.BlockSpec((f, d), lambda i: (i, 0))
    return pl.pallas_call(
        finish_kernel,
        grid=(n // f,),
        in_specs=[row, row, hbm, hbm],
        out_specs=[pl.BlockSpec((d, f), lambda i: (0, first + i)), pl.BlockSpec((f, d), lambda i: (first + i, 0))],
        out_shape=[jax.ShapeDtypeStruct(dw1.shape, F32), jax.ShapeDtypeStruct(dw2.shape, F32)],
        input_output_aliases={2: 0, 3: 1},
        compiler_params=pltpu.CompilerParams(vmem_limit_bytes=VMEM_BYTES, dimension_semantics=("arbitrary",)),
        cost_estimate=pl.CostEstimate(flops=n * d, bytes_accessed=16 * n * d, transcendentals=0),
        name="finish",
    )(s1, s2, dw1, dw2)


def solution(mesh):
    def body(x, g, w1, w2):
        w1, w2 = w1[0, 0], w2[0, 0]
        ff, d = w2.shape
        nz = NB * 512
        fs = (ff - nz) // 16
        at = nz + lax.axis_index("inner") * fs
        w1t = lax.dynamic_slice(w1, (0, at), (d, fs)).T
        w2s = lax.dynamic_slice(w2, (at, 0), (fs, d))
        y, dx, h, gg, z = fb(x[0], g[0], w1, w2, nz)
        s1, s2 = share(w1t, w2s, h, gg)
        s1 = lax.all_gather(s1, "inner", axis=0, tiled=True)
        s2 = lax.all_gather(s2, "inner", axis=0, tiled=True)
        dw1, dw2 = wgrad(z, w2, h, gg)
        dw1, dw2 = finish(s1, s2, dw1, dw2, NB)
        return y[None], dx[None], dw1[None, None], dw2[None, None]

    tok = P(("data", "stage"), "inner", None)
    wsp = P(None, "stage", None, None)
    dsp = P("data", "stage", None, None)
    return jax.shard_map(body, mesh=mesh, in_specs=(tok, tok, wsp, wsp), out_specs=(tok, tok, dsp, dsp), check_vma=False)
```

time: 607 us -> 511 us (0.84)
  Pallas kernels: 600 us -> 483 us
  between operations: 0.83 us -> 14.3 us
    pallas_call x1 -> x3, Pallas kernels: 341 us -> 228 us  [the longest x1 196 us: wgrad(): pl.pallas_call(wgrad_kernel, grid=(nb,), in_specs=[hbm, pl.BlockSpec((f,...]
  transfers between devices with their start and end apart: 0 -> 2, of which waited for: 0 -> 0; matrix products, arithmetic and copies ran while one was open for 0% -> 0% of each run, Pallas kernels for 0% -> 39%
where the time goes in v2:
time: 511 us; the launch traced here: 505 us
  Pallas kernels  483 us (95%)
  between operations  14.3 us (3%)
  local copies, waits for them, and re-layouts  6.97 us (1%)
    pallas_call x1, Pallas kernels, fb(): pl.pallas_call(functools.partial(fb_kernel, ns=ns), in_specs=[vm, vm, hbm...  255 us
    pallas_call x1, Pallas kernels, wgrad(): pl.pallas_call(wgrad_kernel, grid=(nb,), in_specs=[hbm, pl.BlockSpec((f,...  196 us
    pallas_call x1, Pallas kernels, share(): pl.pallas_call(functools.partial(share_kernel, tc=tc), in_specs=[vm, vm,...  17.4 us
    pallas_call x1, Pallas kernels, finish(): pl.pallas_call(finish_kernel, grid=(n // f,), in_specs=[row, row, hbm, hb...  14.8 us
  transfers between devices with their start and end apart: 2, of which 0 were waited for; matrix products, arithmetic and copies ran while one was open for 0% of the time, Pallas kernels for 39%

profile of v2, /device:TPU:0, one launch (start us, length us, event | category | flops | bytes accessed | tf_op | source)
XLA Modules:
  0.0 505.3 jit_solution(5212126810277283278)
XLA Ops:
  7.2 0.0 all-gather.3.cloned.1.call-start
  7.2 1.7 dynamic-slice_bitcast_fusion.w2
  8.9 1.3 constant_dynamic-slice_fusion
  10.2 0.9 copy.10
  11.1 255.0 %fb.1 = (bf16[32,1536]{1,0:T(8,128)(2,1)}, bf16[32,1536]{1,0:T(8,128)(2,1)}, bf16[4,4,2,128,1536]{4,3,2,1,0:T(8,128)(2,1)}, bf16[4,4,2,128,1536]{4,3,2,1,0:T(8,128)(2,1)}, f32[4608,4096]{1,0:T(8,128)}) custom-call(bf16[32,1536]{1,0:T(8,128)(2,1)} %bitcast.21, bf16[32,1536]{1,0:T(8,128)(2,1)} %bitcast.22, bf16[1536,6144]{1,0:T(8,128)(2,1)} %bitcast.17, ...), custom_call_target="tpu_custom_call" | custom-call | tf_op jit(solution)/shard_map/fb/pallas_call | solution.py:423
  266.1 17.4 %share.1 = (f32[96,1536]{1,0:T(8,128)}, f32[96,1536]{1,0:T(8,128)}) custom-call(bf16[96,1536]{1,0:T(8,128)(2,1)} %bitcast.20, bf16[96,1536]{1,0:T(8,128)(2,1)} %dynamic-slice_bitcast_fusion.w2, bf16[4096,1536]{1,0:T(8,128)(2,1)} %bitcast.25, bf16[4096,1536]{1,0:T(8,128)(2,1)} %bitcast.27), custom_call_target="tpu_custom_call" | custom-call | flops 9663676416 | bytes 25165824 | tf_op jit(solution)/shard_map/share/pallas_call | solution.py:563
  283.5 0.0 all-gather.3.cloned.1.call-update
  283.5 0.0 all-gather.5.cloned.1.call-start
  283.6 0.7 all-gather.5.cloned.1.call-update
  284.3 196.1 %wgrad.1 = (f32[1536,6144]{1,0:T(8,128)}, f32[6144,1536]{1,0:T(8,128)}) custom-call(f32[4608,4096]{1,0:T(8,128)} %get-tuple-element.21.z_hbm, bf16[6144,1536]{1,0:T(8,128)(2,1)} %bitcast.19, bf16[4096,1536]{1,0:T(8,128)(2,1)} %bitcast.26, bf16[4096,1536]{1,0:T(8,128)(2,1)} %bitcast.28), custom_call_target="tpu_custom_call" | custom-call | flops 231928233984 | bytes 220200960 | tf_op jit(solution)/shard_map/wgrad/pallas_call | solution.py:514
  480.4 0.0 all-gather.3.cloned.1.call-done.s1
  480.4 0.0 all-gather.5.cloned.1.call-done.s2
  480.4 14.8 %finish.1 = (f32[1536,6144]{1,0:T(8,128)}, f32[6144,1536]{1,0:T(8,128)}) custom-call(f32[1536,1536]{1,0:T(8,128)} %all-gather.3.cloned.1.call-done.s1, f32[1536,1536]{1,0:T(8,128)} %all-gather.5.cloned.1.call-done.s2, f32[1536,6144]{1,0:T(8,128)} %get-tuple-element.22.dw1_in, ...), custom_call_target="tpu_custom_call", output_to_operand_aliasing={{0}: (2, {}), {1}: (3, {})} | custom-call | flops 2359296 | bytes 37748736 | tf_op jit(solution)/shard_map/finish/pallas_call | solution.py:586
  495.2 1.5 copy.15
  496.7 1.5 copy.16
Async XLA Ops:
  7.2 473.2 %all-gather.3.cloned.1.call-start = ((), (), s32[]{:S(2)}) async-start(), calls=%async_computation | async-start | bytes 10027008 | tf_op jit(solution)/shard_map/all_gather | solution.py:610
  283.5 196.9 %all-gather.5.cloned.1.call-start = ((), (), s32[]{:S(2)}) async-start(), calls=%async_computation.1 | async-start | bytes 10027008 | tf_op jit(solution)/shard_map/all_gather | solution.py:611
Sparse Core Ops, SparseCore 0:
  283.7 72.7 all-gather.2
  358.6 75.1 all-gather.4

commit v3 on v2

--- a/solution.py
+++ b/solution.py
@@ -13,7 +13,6 @@
 C0 = 0.7978845608028654
 C1 = 0.044715
 VMEM_BYTES = 67043328
-PRE = 3
 NB = 9
 
 
@@ -292,97 +291,118 @@
         ag_go(H, 2)
 
     nf = zall.shape[0] // 512
-    nt_z = zall.shape[1] // 512
     zb = (zb0, zb1, zb2)
 
-    def hload(t):
+    def line_of(t):
+        c = jnp.where((t == 1) | (t == 4) | (t == 5) | (t == 7), 1, 0)
+        off = jnp.where(t < 2, 0, jnp.where(t >= 6, 2, jnp.where(lax.rem(t, 2) == 0, 1, 3)))
+        return c, lax.rem(jnp.where(c == 0, y, z) + off, 4)
+
+    def hload(t, k):
+        _, l = line_of(t)
         s = lax.rem(t, 2)
-        return pltpu.make_async_copy(hall.at[t // 2, pl.ds(2 * s, 2)], hbuf.at[s], hsem.at[s])
-
-    def zput(n, u):
-        rows = pl.ds(pl.multiple_of(lax.rem(n, nf) * 512, 512), 512)
-        cols = pl.ds(pl.multiple_of((n // nf) * 512, 512), 512)
+        src = hall.at[:, l, 0] if k == 0 else hall.at[l, :, 1]
+        return pltpu.make_async_copy(src, hbuf.at[s], hsem.at[s])
+
+    def hstart(t):
+        for k in (0, 1):
+            @pl.when(line_of(t)[0] == k)
+            def _():
+                hload(t, k).start()
+
+    def zput(t, j, u):
+        c, l = line_of(t)
+        rows = pl.ds(pl.multiple_of(j * 512, 512), 512)
+        cols = pl.ds(pl.multiple_of((c * 4 + l) * 512, 512), 512)
         return pltpu.make_async_copy(zb[u], zall.at[rows, cols], zsem.at[u])
 
     def zwork(t0, t1):
-        hload(t0).start()
+        hstart(t0)
 
         @pl.loop(t0, t1)
         def _(t):
-            hload(t).wait()
+            hload(t, 0).wait()
 
             @pl.when(t + 1 < t1)
             def _():
-                hload(t + 1).start()
+                hstart(t + 1)
 
             @pl.loop(0, nf // 3)
             def _(k):
                 for u in range(3):
-                    n = t * nf + 3 * k + u
-
-                    @pl.when(n >= t0 * nf + 3)
+                    j = 3 * k + u
+
+                    @pl.when((t > t0) | (k > 0))
                     def _():
-                        zput(n - 3, u).wait()
-                    rows = pl.ds(pl.multiple_of((3 * k + u) * 512, 512), 512)
+                        zput(t, j, u).wait()
+                    rows = pl.ds(pl.multiple_of(j * 512, 512), 512)
                     hc = hbuf[lax.rem(t, 2)].reshape(512, d)
                     zb[u][...] = lax.dot_general(bufb[rows, :], hc, NT, preferred_element_type=F32)
-                    zput(n, u).start()
+                    zput(t, j, u).start()
         for u in range(3):
-            zput(t1 * nf - 3 + u, u).wait()
-
-    pre = jnp.where(p < 2, PRE, 0)
-    mid = jnp.where(p < 2, (nt_z + PRE) // 2, nt_z // 2)
-
-    @pl.when(p < 4)
-    def _():
-        ag_go(H, 3)
-
-    @pl.when(p < 2)
-    def _():
-        ag_end(H)
-        zwork(0, pre)
-
-    @pl.when(p < last)
-    def _():
-        @pl.loop(0, 2)
-        def _(c):
-            hop_b(c).wait_recv()
-            ag_in(G, c)
-            bwd(c)
-
-            @pl.when(p > 0)
-            def _():
-                hop_b(c).start()
+            zput(t0, u, u).wait()
+
+    pre = jnp.where(p < 2, 8, jnp.where(p < 5, 10 - 2 * p, 0))
+
+    @pl.loop(0, 6)
+    def _(ph):
+        @pl.when((ph == 1) & (p < 4))
+        def _():
+            ag_go(H, 3)
+
+        @pl.when((ph == 2) & (p < 2))
+        def _():
+            ag_end(H)
+
+        @pl.when((ph == 3) & (p < last))
+        def _():
+            @pl.loop(0, 2)
+            def _(c):
+                hop_b(c).wait_recv()
+                ag_in(G, c)
+                bwd(c)
+
+                @pl.when(p > 0)
+                def _():
+                    hop_b(c).start()
+
+                @pl.when(p == 0)
+                def _():
+                    for m in range(nmb):
+                        @pl.when(c * nmb + m > 0)
+                        def _():
+                            put_dx(c, m).start()
 
             @pl.when(p == 0)
             def _():
-                for m in range(nmb):
-                    @pl.when(c * nmb + m > 0)
-                    def _():
-                        put_dx(c, m).start()
-
-        @pl.when(p == 0)
-        def _():
-            pltpu.make_async_copy(gout.at[0, pl.ds(0, sub)], dx_ref, dr).start()
-        ag_in_end(G)
-
-    @pl.when(p >= 4)
-    def _():
-        ag_go(H, 3)
-
-    @pl.when(p >= 2)
-    def _():
-        ag_end(H)
-
-    @pl.when(p < last)
-    def _():
-        ag_go(G, 2)
-    zwork(pre, mid)
-
-    @pl.when(p < last)
-    def _():
-        ag_go(G, 3)
-    zwork(mid, nt_z)
+                pltpu.make_async_copy(gout.at[0, pl.ds(0, sub)], dx_ref, dr).start()
+            ag_in_end(G)
+
+        @pl.when((ph == 4) & (p >= 4))
+        def _():
+            ag_go(H, 3)
+
+        @pl.when((ph == 4) & (p < last))
+        def _():
+            ag_go(G, 2)
+
+        @pl.when((ph == 5) & (p >= 2))
+        def _():
+            ag_end(H)
+
+        @pl.when((ph == 5) & (p < last))
+        def _():
+            ag_go(G, 3)
+
+        k = lax.rem(ph, 3)
+        edge = jnp.where(k == 0, 0, jnp.where(k == 1, 2, 6))
+        edge1 = jnp.where(k == 0, 2, jnp.where(k == 1, 6, 8))
+        lo = jnp.where(ph < 3, edge, jnp.maximum(edge, pre))
+        hi = jnp.where(ph < 3, jnp.minimum(edge1, pre), edge1)
+
+        @pl.when(lo < hi)
+        def _():
+            zwork(lo, hi)
     ag_end(G)
 
     @pl.when(p > 0)
@@ -428,23 +448,22 @@
         scratch_shapes=[
             pltpu.VMEM((d, f), BF), pltpu.VMEM((f, d), BF), pltpu.VMEM((2 * ck, f), F32), pltpu.VMEM((3, ck, f), BF),
             pltpu.VMEM((2, ck, d), BF), pltpu.VMEM((2, ck, d), BF), pltpu.VMEM((2, ck, d), BF), pltpu.VMEM((2, ck, d), BF),
-            pltpu.VMEM((2, d, 512), BF), pltpu.VMEM((2, 2, 2, ck, d), BF), pltpu.VMEM((512, 512), F32), pltpu.VMEM((512, 512), F32), pltpu.VMEM((512, 512), F32),
+            pltpu.VMEM((2, d, 512), BF), pltpu.VMEM((2, 4, ck, d), BF), pltpu.VMEM((512, 512), F32), pltpu.VMEM((512, 512), F32), pltpu.VMEM((512, 512), F32),
             dma((2,)), dma((2,)), dma((2,)), dma((3,)), dma, dma((ns,)), dma, dma((ns,)), dma((2,)), dma((2,)), dma((2,)), dma((2,)),
             dma((ns,)), dma, dma((ns,)), dma, dma((4,)), dma((32,)), dma((32,)),
         ],
         compiler_params=pltpu.CompilerParams(vmem_limit_bytes=VMEM_BYTES, collective_id=0, has_side_effects=True),
         name="fb",
     )(x, g, w1, w2)
-    return y, dx, h.reshape(-1, d), gg.reshape(-1, d), z
+    return y, dx, h, gg, z
 
 
 def wgrad_kernel(z_hbm, w2_ref, h_hbm, g_hbm, dw1_ref, dw2_ref, h_ref, g_ref, at, dzt, z0, z1, d0, d1, hsem, zsem):
     b = pl.program_id(0)
     nb = pl.num_programs(0)
-    t, d = h_ref.shape
-    f = w2_ref.shape[0]
-    tc = d0.shape[1]
-    n = t // tc
+    n, d = h_ref.shape[0], h_ref.shape[3]
+    f, tc = d0.shape
+    t = n * tc
     half = t // 2
     zs, ds = (z0, z1), (d0, d1)
 
@@ -452,20 +471,22 @@
         rows = pl.ds(pl.multiple_of(blk * f, f), f)
         return pltpu.make_async_copy(z_hbm.at[rows, pl.ds(i * half, half)], zs[i], zsem.at[i])
 
-    gget = pltpu.make_async_copy(g_hbm, g_ref, hsem.at[0])
-    hget = pltpu.make_async_copy(h_hbm, h_ref, hsem.at[1])
+    def get(src, dst, i, k):
+        return pltpu.make_async_copy(src.at[:, i, 0] if i < 4 else src.at[i - 4, :, 1], dst.at[i], hsem.at[k, i])
 
     @pl.when(b == 0)
     def _():
-        gget.start()
+        for i in range(n):
+            get(g_hbm, g_ref, i, 0).start()
         zget(0, 0).start()
         zget(0, 1).start()
-        hget.start()
-        gget.wait()
+        for i in range(n):
+            get(h_hbm, h_ref, i, 1).start()
+        for i in range(n):
+            get(g_hbm, g_ref, i, 0).wait()
 
     def dots(i):
-        rows = pl.ds(i * tc, tc)
-        ds[i % 2][...] = lax.dot_general(w2_ref[...], g_ref[rows, :], NT, preferred_element_type=F32)
+        ds[i % 2][...] = lax.dot_general(w2_ref[...], g_ref[i].reshape(tc, d), NT, preferred_element_type=F32)
 
     def elem(i):
         cols = pl.ds(i * tc, tc)
@@ -488,17 +509,18 @@
 
     @pl.when(b == 0)
     def _():
-        hget.wait()
+        for i in range(n):
+            get(h_hbm, h_ref, i, 1).wait()
     for i in range(n // 2 + 1, n):
         dots(i)
         elem(i - 1)
     elem(n - 1)
     for j in range(0, d, 512):
         cols = pl.ds(j, 512)
-        p1 = jnp.dot(dzt[...], h_ref[:, cols], preferred_element_type=F32)
+        p1 = jnp.dot(dzt[...], h_ref[:, :, :, cols].reshape(t, 512), preferred_element_type=F32)
         for r in range(0, 512, 128):
             dw1_ref[pl.ds(j + r, 128), :] = p1[:, r:r + 128].T
-        dw2_ref[:, cols] = jnp.dot(at[...], g_ref[:, cols], preferred_element_type=F32)
+        dw2_ref[:, cols] = jnp.dot(at[...], g_ref[:, :, :, cols].reshape(t, 512), preferred_element_type=F32)
 
     @pl.when(b + 1 < nb)
     def _():
@@ -507,8 +529,9 @@
 
 def wgrad(z, w2, h, g, f=512, tc=512):
     ff, d = w2.shape
-    t = h.shape[0]
+    t = z.shape[1]
     nb = z.shape[0] // f
+    kept = pltpu.VMEM((t // tc, 4, tc // 4, d), BF)
     hbm = pl.BlockSpec(memory_space=pl.ANY)
     dma = pltpu.SemaphoreType.DMA
     return pl.pallas_call(
@@ -517,8 +540,8 @@
         in_specs=[hbm, pl.BlockSpec((f, d), lambda i: (i, 0)), hbm, hbm],
         out_specs=[pl.BlockSpec((d, f), lambda i: (0, i)), pl.BlockSpec((f, d), lambda i: (i, 0))],
         out_shape=[jax.ShapeDtypeStruct((d, ff), F32), jax.ShapeDtypeStruct((ff, d), F32)],
-        scratch_shapes=[pltpu.VMEM((t, d), BF)] * 2 + [pltpu.VMEM((f, t), BF)] * 2 + [pltpu.VMEM((f, t // 2), F32)] * 2 + [pltpu.VMEM((f, tc), F32)] * 2
-        + [dma((2,)), dma((2,))],
+        scratch_shapes=[kept] * 2 + [pltpu.VMEM((f, t), BF)] * 2 + [pltpu.VMEM((f, t // 2), F32)] * 2 + [pltpu.VMEM((f, tc), F32)] * 2
+        + [dma((2, t // tc)), dma((2,))],
         compiler_params=pltpu.CompilerParams(vmem_limit_bytes=VMEM_BYTES, dimension_semantics=("arbitrary",)),
         cost_estimate=pl.CostEstimate(flops=6 * t * d * ff, bytes_accessed=10 * d * ff + 4 * t * d + 4 * t * ff, transcendentals=t * ff),
         name="wgrad",
@@ -606,7 +629,7 @@
         w1t = lax.dynamic_slice(w1, (0, at), (d, fs)).T
         w2s = lax.dynamic_slice(w2, (at, 0), (fs, d))
         y, dx, h, gg, z = fb(x[0], g[0], w1, w2, nz)
-        s1, s2 = share(w1t, w2s, h, gg)
+        s1, s2 = share(w1t, w2s, h.reshape(-1, d), gg.reshape(-1, d))
         s1 = lax.all_gather(s1, "inner", axis=0, tiled=True)
         s2 = lax.all_gather(s2, "inner", axis=0, tiled=True)
         dw1, dw2 = wgrad(z, w2, h, gg)

time: 511 us -> 504 us (0.986); the launches traced: 505 us -> 504 us
    pallas_call x1, Pallas kernels: 255 us -> 240 us  [fb(): pl.pallas_call(functools.partial(fb_kernel, ns=ns), in_specs=[vm, vm, hbm...]
    pallas_call x1, Pallas kernels: 196 us -> 210 us  [wgrad(): pl.pallas_call(wgrad_kernel, grid=(nb,), in_specs=[hbm, pl.BlockSpec((f,...]
  transfers between devices with their start and end apart: 2 -> 2, of which waited for: 0 -> 0; matrix products, arithmetic and copies ran while one was open for 0% -> 0% of each run, Pallas kernels for 39% -> 42%
where the time goes in v3:
time: 504 us
  Pallas kernels  482 us (96%)
  between operations  14.3 us (3%)
  local copies, waits for them, and re-layouts  6.97 us (1%)
    pallas_call x1, Pallas kernels, fb(): pl.pallas_call(functools.partial(fb_kernel, ns=ns), in_specs=[vm, vm, hbm...  240 us
    pallas_call x1, Pallas kernels, wgrad(): pl.pallas_call(wgrad_kernel, grid=(nb,), in_specs=[hbm, pl.BlockSpec((f,...  210 us
    pallas_call x1, Pallas kernels, share(): pl.pallas_call(functools.partial(share_kernel, tc=tc), in_specs=[vm, vm,...  17.4 us
    pallas_call x1, Pallas kernels, finish(): pl.pallas_call(finish_kernel, grid=(n // f,), in_specs=[row, row, hbm, hb...  14.8 us
  transfers between devices with their start and end apart: 2, of which 0 were waited for; matrix products, arithmetic and copies ran while one was open for 0% of the time, Pallas kernels for 42%

profile of v3, /device:TPU:0, one launch (start us, length us, event | category | flops | bytes accessed | tf_op | source)
XLA Modules:
  0.0 503.9 jit_solution(8506801207455142029)
XLA Ops:
  7.2 0.0 all-gather.3.cloned.1.call-start
  7.2 1.7 dynamic-slice_bitcast_fusion.w2
  8.9 1.3 constant_dynamic-slice_fusion
  10.2 0.9 copy.10
  11.1 240.0 %fb.1 = (bf16[32,1536]{1,0:T(8,128)(2,1)}, bf16[32,1536]{1,0:T(8,128)(2,1)}, bf16[4,4,2,128,1536]{4,3,2,1,0:T(8,128)(2,1)}, bf16[4,4,2,128,1536]{4,3,2,1,0:T(8,128)(2,1)}, f32[4608,4096]{1,0:T(8,128)}) custom-call(bf16[32,1536]{1,0:T(8,128)(2,1)} %bitcast.21, bf16[32,1536]{1,0:T(8,128)(2,1)} %bitcast.22, bf16[1536,6144]{1,0:T(8,128)(2,1)} %bitcast.17, ...), custom_call_target="tpu_custom_call" | custom-call | tf_op jit(solution)/shard_map/fb/pallas_call | solution.py:443
  251.1 17.4 %share.1 = (f32[96,1536]{1,0:T(8,128)}, f32[96,1536]{1,0:T(8,128)}) custom-call(bf16[96,1536]{1,0:T(8,128)(2,1)} %bitcast.20, bf16[96,1536]{1,0:T(8,128)(2,1)} %dynamic-slice_bitcast_fusion.w2, bf16[4096,1536]{1,0:T(8,128)(2,1)} %bitcast.25, bf16[4096,1536]{1,0:T(8,128)(2,1)} %bitcast.26), custom_call_target="tpu_custom_call" | custom-call | flops 9663676416 | bytes 25165824 | tf_op jit(solution)/shard_map/share/pallas_call | solution.py:586
  268.5 0.0 all-gather.3.cloned.1.call-update
  268.5 0.0 all-gather.5.cloned.1.call-start
  268.6 0.7 all-gather.5.cloned.1.call-update
  269.3 209.7 %wgrad.1 = (f32[1536,6144]{1,0:T(8,128)}, f32[6144,1536]{1,0:T(8,128)}) custom-call(f32[4608,4096]{1,0:T(8,128)} %get-tuple-element.21.z_hbm, bf16[6144,1536]{1,0:T(8,128)(2,1)} %bitcast.19, bf16[4,4,2,128,1536]{4,3,2,1,0:T(8,128)(2,1)} %get-tuple-element.17.h_hbm, bf16[4,4,2,128,1536]{4,3,2,1,0:T(8,128)(2,1)} %get-tuple-element.18.g_hbm), custom_call_target="tpu_custom_call" | custom-call | flops 231928233984 | bytes 220200960 | tf_op jit(solution)/shard_map/wgrad/pallas_call | solution.py:537
  478.9 0.0 all-gather.3.cloned.1.call-done.s1
  479.0 0.0 all-gather.5.cloned.1.call-done.s2
  479.0 14.8 %finish.1 = (f32[1536,6144]{1,0:T(8,128)}, f32[6144,1536]{1,0:T(8,128)}) custom-call(f32[1536,1536]{1,0:T(8,128)} %all-gather.3.cloned.1.call-done.s1, f32[1536,1536]{1,0:T(8,128)} %all-gather.5.cloned.1.call-done.s2, f32[1536,6144]{1,0:T(8,128)} %get-tuple-element.22.dw1_in, ...), custom_call_target="tpu_custom_call", output_to_operand_aliasing={{0}: (2, {}), {1}: (3, {})} | custom-call | flops 2359296 | bytes 37748736 | tf_op jit(solution)/shard_map/finish/pallas_call | solution.py:609
  493.8 1.5 copy.15
  495.3 1.5 copy.16
Async XLA Ops:
  7.2 471.8 %all-gather.3.cloned.1.call-start = ((), (), s32[]{:S(2)}) async-start(), calls=%async_computation | async-start | bytes 10027008 | tf_op jit(solution)/shard_map/all_gather | solution.py:633
  268.5 210.5 %all-gather.5.cloned.1.call-start = ((), (), s32[]{:S(2)}) async-start(), calls=%async_computation.1 | async-start | bytes 10027008 | tf_op jit(solution)/shard_map/all_gather | solution.py:634
Sparse Core Ops, SparseCore 0:
  268.6 72.2 all-gather.2
  343.1 75.2 all-gather.4

commit v4 on v3

--- a/solution.py
+++ b/solution.py
@@ -14,6 +14,7 @@
 C1 = 0.044715
 VMEM_BYTES = 67043328
 NB = 9
+BLK = 512
 
 
 def gelu_parts(z):
@@ -36,10 +37,10 @@
     hf = ck // 2
 
     def at_stage(s):
-        return {"data": 0, "inner": q, "stage": s}
+        return {"inner": q, "stage": s}
 
     def at_plane(zz, yy):
-        return {"data": 0, "inner": zz * 4 + yy, "stage": p}
+        return {"inner": zz * 4 + yy, "stage": p}
 
     def rc(src, dst, ss, rs, dev):
         return pltpu.make_async_remote_copy(src_ref=src, dst_ref=dst, send_sem=ss, recv_sem=rs, device_id=dev, device_id_type=MESH)
@@ -82,11 +83,15 @@
     def _():
         gin[1, ck - sub:] = g_ref[...]
 
-    def hop_f(c):
-        return rc(hout.at[c], hin.at[c], fs.at[c], fr.at[c], at_stage(lax.rem(p + 1, ns)))
-
-    def hop_b(c):
-        return rc(gout.at[c], gin.at[c], bs.at[c], br.at[c], at_stage(lax.rem(p + ns - 1, ns)))
+    def hop_f(c, k):
+        cols = pl.ds(k * BLK, BLK)
+        return rc(hout.at[c, :, cols], hin.at[c, :, cols], fs.at[c, k], fr.at[c, k], at_stage(lax.rem(p + 1, ns)))
+
+    def hop_b(c, k):
+        cols = pl.ds(k * BLK, BLK)
+        return rc(gout.at[c, :, cols], gin.at[c, :, cols], bs.at[c, k], br.at[c, k], at_stage(lax.rem(p + ns - 1, ns)))
+
+    nk = d // BLK
 
     def put_y(c, m):
         return rc(hout.at[c, pl.ds(m * sub, sub)], y_ref, ys.at[c * nmb + m], yr, at_stage(c * nmb + m))
@@ -158,49 +163,56 @@
             own(*who, c).wait()
         ag_go(who, 1)
 
-    def up(c, src, k):
-        for j in range(0, d, 512):
-            u = jnp.dot(act[k], bufb[:, j:j + 512], preferred_element_type=F32)
-            hout[c, :, j:j + 512] = (src[:, j:j + 512].astype(F32) + u).astype(BF)
 
     def rows_of(c, r, n):
         return pl.ds(pl.multiple_of(c * ck + r, n), n)
 
     def fwd(c):
         h = hin.at[c]
-        for j in range(0, f, 512):
-            zz = jnp.dot(h[...], bufa[:, j:j + 512], preferred_element_type=F32)
+        for j in range(0, f, BLK):
+            zz = jnp.dot(h[...], bufa[:, j:j + BLK], preferred_element_type=F32)
             for r in range(0, ck, 32):
                 a_, d_ = gelu_parts(zz[r:r + 32])
-                act[0, r:r + 32, j:j + 512] = a_.astype(BF)
-                dg[rows_of(c, r, 32), j:j + 512] = d_
+                act[0, r:r + 32, j:j + BLK] = a_.astype(BF)
+                dg[rows_of(c, r, 32), j:j + BLK] = d_
 
         @pl.when(c == 0)
         def _():
             cw2.wait()
-        up(c, h, 0)
+        for k in range(nk):
+            cols = pl.ds(k * BLK, BLK)
+            u = jnp.dot(act[0], bufb[:, cols], preferred_element_type=F32)
+            hout[c, :, cols] = (h[:, cols].astype(F32) + u).astype(BF)
+            hop_f(c, k).start()
 
     def bwd(c):
         g = gin.at[c]
-        for j in range(0, f, 512):
-            da = jnp.dot(g[...], bufa[:, j:j + 512], preferred_element_type=F32)
+        for j in range(0, f, BLK):
+            da = jnp.dot(g[...], bufa[:, j:j + BLK], preferred_element_type=F32)
             for r in range(0, ck, 32):
-                act[0, r:r + 32, j:j + 512] = (da[r:r + 32] * dg[rows_of(c, r, 32), j:j + 512]).astype(BF)
-        for j in range(0, d, 512):
-            u = jnp.dot(act[0], bufb[:, j:j + 512], preferred_element_type=F32)
-            gout[c, :, j:j + 512] = (g[:, j:j + 512].astype(F32) + u).astype(BF)
+                act[0, r:r + 32, j:j + BLK] = (da[r:r + 32] * dg[rows_of(c, r, 32), j:j + BLK]).astype(BF)
+        for k in range(nk):
+            cols = pl.ds(k * BLK, BLK)
+            u = jnp.dot(act[0], bufb[:, cols], preferred_element_type=F32)
+            gout[c, :, cols] = (g[:, cols].astype(F32) + u).astype(BF)
+
+            @pl.when(p > 0)
+            def _():
+                hop_b(c, k).start()
 
     def turn(c):
         h, g = hin.at[c], gin.at[c]
-        for j in range(0, f, 512):
-            zz = jnp.dot(h[...], bufa[:, j:j + 512], preferred_element_type=F32)
+        for j in range(0, f, BLK):
+            zz = jnp.dot(h[...], bufa[:, j:j + BLK], preferred_element_type=F32)
             for r in range(0, ck, 32):
                 a_, d_ = gelu_parts(zz[r:r + 32])
-                act[c, r:r + 32, j:j + 512] = a_.astype(BF)
-                act[2, r:r + 32, j:j + 512] = (dg[rows_of(c, r, 32), j:j + 512] * d_).astype(BF)
-        for j in range(0, d, 512):
-            u = lax.dot_general(act[2], bufa[j:j + 512, :], NT, preferred_element_type=F32)
-            gout[c, :, j:j + 512] = (g[:, j:j + 512].astype(F32) + u).astype(BF)
+                act[c, r:r + 32, j:j + BLK] = a_.astype(BF)
+                act[2, r:r + 32, j:j + BLK] = (dg[rows_of(c, r, 32), j:j + BLK] * d_).astype(BF)
+        for k in range(nk):
+            cols = pl.ds(k * BLK, BLK)
+            u = lax.dot_general(act[2], bufa[cols, :], NT, preferred_element_type=F32)
+            gout[c, :, cols] = (g[:, cols].astype(F32) + u).astype(BF)
+            hop_b(c, k).start()
 
     cw1.wait()
 
@@ -217,10 +229,10 @@
 
             @pl.when(p > 0)
             def _():
-                hop_f(c).wait_recv()
+                for k in range(nk):
+                    hop_f(c, k).wait_recv()
             ag_in(H, c)
             fwd(c)
-            hop_f(c).start()
         ag_in_end(H)
 
     @pl.when(p == last)
@@ -234,8 +246,11 @@
 
         @pl.loop(0, 2)
         def _(c):
-            for j in range(0, f, 512):
-                dg[rows_of(c, 0, ck), j:j + 512] = lax.dot_general(gin[c], bufb[j:j + 512, :], NT, preferred_element_type=F32)
+            @pl.loop(0, f // 1024)
+            def _(i):
+                for r in (0, BLK):
+                    js = pl.ds(pl.multiple_of(i * 1024 + r, BLK), BLK)
+                    dg[rows_of(c, 0, ck), js] = lax.dot_general(gin[c], bufb[js, :], NT, preferred_element_type=F32)
         for c in (0, 1):
             own(*G, c).wait()
         for step in (1, 2, 3):
@@ -243,14 +258,18 @@
 
         @pl.loop(0, 2)
         def _(c):
-            hop_f(c).wait_recv()
+            for k in range(nk):
+                hop_f(c, k).wait_recv()
             ag_in(H, c)
             turn(c)
-            hop_b(c).start()
 
         @pl.loop(0, 2)
         def _(c):
-            up(c, hin.at[c], c)
+            @pl.loop(0, nk)
+            def _(k):
+                cols = pl.ds(pl.multiple_of(k * BLK, BLK), BLK)
+                u = jnp.dot(act[c], bufb[:, cols], preferred_element_type=F32)
+                hout[c, :, cols] = (hin[c, :, cols].astype(F32) + u).astype(BF)
             for m in range(nmb):
                 @pl.when(c * nmb + m < last)
                 def _():
@@ -263,7 +282,7 @@
     def _():
         ag_go(H, 2)
 
-    nt = 512
+    nt = BLK
 
     def tload(i, s):
         return pltpu.make_async_copy(w1_hbm.at[:, pl.ds(pl.multiple_of(i * nt, nt), nt)], tmp.at[s], tsem.at[s])
@@ -290,7 +309,7 @@
     def _():
         ag_go(H, 2)
 
-    nf = zall.shape[0] // 512
+    nf = zall.shape[0] // BLK
     zb = (zb0, zb1, zb2)
 
     def line_of(t):
@@ -312,8 +331,8 @@
 
     def zput(t, j, u):
         c, l = line_of(t)
-        rows = pl.ds(pl.multiple_of(j * 512, 512), 512)
-        cols = pl.ds(pl.multiple_of((c * 4 + l) * 512, 512), 512)
+        rows = pl.ds(pl.multiple_of(j * BLK, BLK), BLK)
+        cols = pl.ds(pl.multiple_of((c * 4 + l) * BLK, BLK), BLK)
         return pltpu.make_async_copy(zb[u], zall.at[rows, cols], zsem.at[u])
 
     def zwork(t0, t1):
@@ -335,8 +354,8 @@
                     @pl.when((t > t0) | (k > 0))
                     def _():
                         zput(t, j, u).wait()
-                    rows = pl.ds(pl.multiple_of(j * 512, 512), 512)
-                    hc = hbuf[lax.rem(t, 2)].reshape(512, d)
+                    rows = pl.ds(pl.multiple_of(j * BLK, BLK), BLK)
+                    hc = hbuf[lax.rem(t, 2)].reshape(BLK, d)
                     zb[u][...] = lax.dot_general(bufb[rows, :], hc, NT, preferred_element_type=F32)
                     zput(t, j, u).start()
         for u in range(3):
@@ -358,13 +377,10 @@
         def _():
             @pl.loop(0, 2)
             def _(c):
-                hop_b(c).wait_recv()
+                for k in range(nk):
+                    hop_b(c, k).wait_recv()
                 ag_in(G, c)
                 bwd(c)
-
-                @pl.when(p > 0)
-                def _():
-                    hop_b(c).start()
 
                 @pl.when(p == 0)
                 def _():
@@ -408,8 +424,9 @@
     @pl.when(p > 0)
     def _():
         gather_x(p).wait_send()
-        hop_b(0).wait_send()
-        hop_b(1).wait_send()
+        for c in (0, 1):
+            for k in range(nk):
+                hop_b(c, k).wait_send()
         put_dx(0, 0).wait_recv()
 
     @pl.when(p == 0)
@@ -421,8 +438,9 @@
     @pl.when(p < ns - 1)
     def _():
         gather_g(p).wait_send()
-        hop_f(0).wait_send()
-        hop_f(1).wait_send()
+        for c in (0, 1):
+            for k in range(nk):
+                hop_f(c, k).wait_send()
         put_y(0, 0).wait_recv()
 
     @pl.when(p == ns - 1)
@@ -436,6 +454,7 @@
     b, d = x.shape
     f = w1.shape[1]
     ck = b * ns // 2
+    nk = d // BLK
     dma = pltpu.SemaphoreType.DMA
     vm = pl.BlockSpec(memory_space=pltpu.VMEM)
     hbm = pl.BlockSpec(memory_space=pl.ANY)
@@ -445,13 +464,16 @@
         in_specs=[vm, vm, hbm, hbm],
         out_specs=[hbm] * 5,
         out_shape=[jax.ShapeDtypeStruct((b, d), BF)] * 2 + [allt] * 2 + [jax.ShapeDtypeStruct((nz, 32 * ck), F32)],
-        scratch_shapes=[
-            pltpu.VMEM((d, f), BF), pltpu.VMEM((f, d), BF), pltpu.VMEM((2 * ck, f), F32), pltpu.VMEM((3, ck, f), BF),
-            pltpu.VMEM((2, ck, d), BF), pltpu.VMEM((2, ck, d), BF), pltpu.VMEM((2, ck, d), BF), pltpu.VMEM((2, ck, d), BF),
-            pltpu.VMEM((2, d, 512), BF), pltpu.VMEM((2, 4, ck, d), BF), pltpu.VMEM((512, 512), F32), pltpu.VMEM((512, 512), F32), pltpu.VMEM((512, 512), F32),
-            dma((2,)), dma((2,)), dma((2,)), dma((3,)), dma, dma((ns,)), dma, dma((ns,)), dma((2,)), dma((2,)), dma((2,)), dma((2,)),
-            dma((ns,)), dma, dma((ns,)), dma, dma((4,)), dma((32,)), dma((32,)),
-        ],
+        scratch_shapes=[pltpu.VMEM((d, f), BF), pltpu.VMEM((f, d), BF), pltpu.VMEM((2 * ck, f), F32), pltpu.VMEM((3, ck, f), BF)]
+        + [pltpu.VMEM((2, ck, d), BF)] * 4
+        + [pltpu.VMEM((2, d, BLK), BF), pltpu.VMEM((2, 4, ck, d), BF)]
+        + [pltpu.VMEM((BLK, BLK), F32)] * 3
+        + [dma((2,))] * 3
+        + [dma((3,))]
+        + [dma, dma((ns,))] * 2
+        + [dma((2, nk))] * 4
+        + [dma((ns,)), dma] * 2
+        + [dma((4,)), dma((32,)), dma((32,))],
         compiler_params=pltpu.CompilerParams(vmem_limit_bytes=VMEM_BYTES, collective_id=0, has_side_effects=True),
         name="fb",
     )(x, g, w1, w2)
@@ -482,7 +504,7 @@
         zget(0, 1).start()
         for i in range(n):
             get(h_hbm, h_ref, i, 1).start()
-        for i in range(n):
+        for i in range(n // 2 + 1):
             get(g_hbm, g_ref, i, 0).wait()
 
     def dots(i):
@@ -509,25 +531,27 @@
 
     @pl.when(b == 0)
     def _():
+        for i in range(n // 2 + 1, n):
+            get(g_hbm, g_ref, i, 0).wait()
         for i in range(n):
             get(h_hbm, h_ref, i, 1).wait()
     for i in range(n // 2 + 1, n):
         dots(i)
         elem(i - 1)
     elem(n - 1)
-    for j in range(0, d, 512):
-        cols = pl.ds(j, 512)
-        p1 = jnp.dot(dzt[...], h_ref[:, :, :, cols].reshape(t, 512), preferred_element_type=F32)
-        for r in range(0, 512, 128):
+    for j in range(0, d, BLK):
+        cols = pl.ds(j, BLK)
+        p1 = jnp.dot(dzt[...], h_ref[:, :, :, cols].reshape(t, BLK), preferred_element_type=F32)
+        for r in range(0, BLK, 128):
             dw1_ref[pl.ds(j + r, 128), :] = p1[:, r:r + 128].T
-        dw2_ref[:, cols] = jnp.dot(at[...], g_ref[:, :, :, cols].reshape(t, 512), preferred_element_type=F32)
+        dw2_ref[:, cols] = jnp.dot(at[...], g_ref[:, :, :, cols].reshape(t, BLK), preferred_element_type=F32)
 
     @pl.when(b + 1 < nb)
     def _():
         zget(b + 1, 1).start()
 
 
-def wgrad(z, w2, h, g, f=512, tc=512):
+def wgrad(z, w2, h, g, f=BLK, tc=BLK):
     ff, d = w2.shape
     t = z.shape[1]
     nb = z.shape[0] // f
@@ -548,9 +572,18 @@
     )(z, w2, h, g)
 
 
-def share_kernel(w1t, w2, h_hbm, g_hbm, s1, s2, h_ref, g_ref, at, dzt, hsem, gsem, *, tc):
+def share_kernel(w1_hbm, w2_hbm, y_in, dx_in, h_hbm, g_hbm, s1, s2, y, dx, h_ref, g_ref, at, dzt, win, wint, w2, hsem, gsem, wsem, *, tc):
     t = h_ref.shape[0]
     n = t // tc
+    fs, ff = w2.shape[0], w2_hbm.shape[0]
+    first = ff - 16 * fs + lax.axis_index("inner") * fs
+    base = jnp.minimum((first // 128) * 128, ff - 256)
+    c1 = pltpu.make_async_copy(w1_hbm.at[:, pl.ds(pl.multiple_of(base, 128), 256)], win, wsem.at[0])
+    c2 = pltpu.make_async_copy(w2_hbm.at[pl.ds(pl.multiple_of(first, 32), fs), :], w2, wsem.at[1])
+    c1.start()
+    c2.start()
+    y[...] = y_in[...]
+    dx[...] = dx_in[...]
 
     def part(src, dst, sem, i):
         rows = pl.ds(i * tc if isinstance(i, int) else pl.multiple_of(i * tc, tc), tc)
@@ -558,6 +591,10 @@
     for i in range(n):
         part(h_hbm, h_ref, hsem, i).start()
         part(g_hbm, g_ref, gsem, i).start()
+    c1.wait()
+    c2.wait()
+    wint[...] = win[...].T
+    w1t = wint.at[pl.ds(pl.multiple_of(first - base, 32), fs), :]
 
     @pl.loop(0, n)
     def _(i):
@@ -570,29 +607,30 @@
         at[:, rows] = a.astype(BF)
         dzt[:, rows] = (da * dg).astype(BF)
 
-    @pl.loop(0, h_ref.shape[1] // 512)
+    @pl.loop(0, h_ref.shape[1] // BLK)
     def _(j):
-        cols = pl.ds(pl.multiple_of(j * 512, 512), 512)
+        cols = pl.ds(pl.multiple_of(j * BLK, BLK), BLK)
         s1[:, cols] = jnp.dot(dzt[...], h_ref[:, cols], preferred_element_type=F32)
         s2[:, cols] = jnp.dot(at[...], g_ref[:, cols], preferred_element_type=F32)
 
 
-def share(w1t, w2, h, g, tc=1024):
-    fs, d = w2.shape
+def share(w1, w2, y, dx, h, g, fs, tc=1024):
+    d = w2.shape[1]
     t = h.shape[0]
     vm = pl.BlockSpec(memory_space=pltpu.VMEM)
     hbm = pl.BlockSpec(memory_space=pl.ANY)
     dma = pltpu.SemaphoreType.DMA
     return pl.pallas_call(
         functools.partial(share_kernel, tc=tc),
-        in_specs=[vm, vm, hbm, hbm],
-        out_specs=[vm, vm],
-        out_shape=[jax.ShapeDtypeStruct((fs, d), F32)] * 2,
-        scratch_shapes=[pltpu.VMEM((t, d), BF)] * 2 + [pltpu.VMEM((fs, t), BF)] * 2 + [dma((t // tc,)), dma((t // tc,))],
+        in_specs=[hbm, hbm, vm, vm, hbm, hbm],
+        out_specs=[vm] * 4,
+        out_shape=[jax.ShapeDtypeStruct((fs, d), F32)] * 2 + [jax.ShapeDtypeStruct(y.shape, BF)] * 2,
+        scratch_shapes=[pltpu.VMEM((t, d), BF)] * 2 + [pltpu.VMEM((fs, t), BF)] * 2
+        + [pltpu.VMEM((d, 256), BF), pltpu.VMEM((256, d), BF), pltpu.VMEM((fs, d), BF), dma((t // tc,)), dma((t // tc,)), dma((2,))],
         compiler_params=pltpu.CompilerParams(vmem_limit_bytes=VMEM_BYTES),
         cost_estimate=pl.CostEstimate(flops=16 * t * d * fs, bytes_accessed=4 * t * d, transcendentals=t * fs),
         name="share",
-    )(w1t, w2, h, g)
+    )(w1, w2, y, dx, h, g)
 
 
 def finish_kernel(s1, s2, dw1_in, dw2_in, dw1, dw2):
@@ -602,8 +640,9 @@
     dw2[...] = s2[...]
 
 
-def finish(s1, s2, dw1, dw2, first, f=512):
+def finish(s1, s2, dw1, dw2, f=256):
     n, d = s1.shape
+    first = dw1.shape[1] // f - n // f
     hbm = pl.BlockSpec(memory_space=pl.ANY)
     row = pl.BlockSpec((f, d), lambda i: (i, 0))
     return pl.pallas_call(
@@ -623,17 +662,14 @@
     def body(x, g, w1, w2):
         w1, w2 = w1[0, 0], w2[0, 0]
         ff, d = w2.shape
-        nz = NB * 512
+        nz = NB * BLK
         fs = (ff - nz) // 16
-        at = nz + lax.axis_index("inner") * fs
-        w1t = lax.dynamic_slice(w1, (0, at), (d, fs)).T
-        w2s = lax.dynamic_slice(w2, (at, 0), (fs, d))
         y, dx, h, gg, z = fb(x[0], g[0], w1, w2, nz)
-        s1, s2 = share(w1t, w2s, h.reshape(-1, d), gg.reshape(-1, d))
+        s1, s2, y, dx = share(w1, w2, y, dx, h.reshape(-1, d), gg.reshape(-1, d), fs)
         s1 = lax.all_gather(s1, "inner", axis=0, tiled=True)
         s2 = lax.all_gather(s2, "inner", axis=0, tiled=True)
         dw1, dw2 = wgrad(z, w2, h, gg)
-        dw1, dw2 = finish(s1, s2, dw1, dw2, NB)
+        dw1, dw2 = finish(s1, s2, dw1, dw2)
         return y[None], dx[None], dw1[None, None], dw2[None, None]
 
     tok = P(("data", "stage"), "inner", None)

time: 504 us -> 493 us (0.978); the launches traced: 504 us -> 484 us
  Pallas kernels: 482 us -> 468 us
  local copies, waits for them, and re-layouts: 6.97 us -> 0 us
    pallas_call x1, Pallas kernels: 210 us -> 199 us  [wgrad(): pl.pallas_call(wgrad_kernel, grid=(nb,), in_specs=[hbm, pl.BlockSpec((f,...]
    pallas_call x1, Pallas kernels: 240 us -> 231 us  [fb(): pl.pallas_call(functools.partial(fb_kernel, ns=ns), in_specs=[vm, vm, hbm...]
    pallas_call x1, Pallas kernels: 17.4 us -> 23.1 us  [share(): pl.pallas_call(functools.partial(share_kernel, tc=tc), in_specs=[hbm, hbm...]
  transfers between devices with their start and end apart: 2 -> 2, of which waited for: 0 -> 0; matrix products, arithmetic and copies ran while one was open for 0% -> 0% of each run, Pallas kernels for 42% -> 41%
where the time goes in v4:
time: 493 us; the launch traced here: 484 us
  Pallas kernels  468 us (95%)
  between operations  14.5 us (3%)
    pallas_call x1, Pallas kernels, fb(): pl.pallas_call(functools.partial(fb_kernel, ns=ns), in_specs=[vm, vm, hbm...  231 us
    pallas_call x1, Pallas kernels, wgrad(): pl.pallas_call(wgrad_kernel, grid=(nb,), in_specs=[hbm, pl.BlockSpec((f,...  199 us
    pallas_call x1, Pallas kernels, share(): pl.pallas_call(functools.partial(share_kernel, tc=tc), in_specs=[hbm, hbm...  23.1 us
    pallas_call x1, Pallas kernels, finish(): pl.pallas_call(finish_kernel, grid=(n // f,), in_specs=[row, row, hbm, hb...  14.6 us
  transfers between devices with their start and end apart: 2, of which 0 were waited for; matrix products, arithmetic and copies ran while one was open for 0% of the time, Pallas kernels for 41%

profile of v4, /device:TPU:0, one launch (start us, length us, event | category | flops | bytes accessed | tf_op | source)
XLA Modules:
  0.0 483.7 jit_solution(10766866861973554979)
XLA Ops:
  7.2 0.0 all-gather.3.cloned.1.call-start
  7.2 231.5 %fb.1 = (bf16[32,1536]{1,0:T(8,128)(2,1)}, bf16[32,1536]{1,0:T(8,128)(2,1)}, bf16[4,4,2,128,1536]{4,3,2,1,0:T(8,128)(2,1)}, bf16[4,4,2,128,1536]{4,3,2,1,0:T(8,128)(2,1)}, f32[4608,4096]{1,0:T(8,128)}) custom-call(bf16[32,1536]{1,0:T(8,128)(2,1)} %bitcast.19, bf16[32,1536]{1,0:T(8,128)(2,1)} %bitcast.20, bf16[1536,6144]{1,0:T(8,128)(2,1)} %bitcast.10, ...), custom_call_target="tpu_custom_call" | custom-call | tf_op jit(solution)/shard_map/fb/pallas_call | solution.py:462
  238.7 23.1 %share.1 = (f32[96,1536]{1,0:T(8,128)}, f32[96,1536]{1,0:T(8,128)}, bf16[32,1536]{1,0:T(8,128)(2,1)}, bf16[32,1536]{1,0:T(8,128)(2,1)}) custom-call(bf16[1536,6144]{1,0:T(8,128)(2,1)} %bitcast.11, bf16[6144,1536]{1,0:T(8,128)(2,1)} %bitcast.13, bf16[32,1536]{1,0:T(8,128)(2,1)} %get-tuple-element.17.y_in, bf16[32,1536]{1,0:T(8,128)(2,1)} %get-tuple-element.18.dx_in, ...), custom_call_target="tpu_custom_call" | custom-call | flops 9663676416 | bytes 25165824 | tf_op jit(solution)/shard_map/share/pallas_call | solution.py:623
  261.8 0.0 all-gather.3.cloned.1.call-update
  261.8 0.0 all-gather.5.cloned.1.call-start
  261.9 0.7 all-gather.5.cloned.1.call-update
  262.6 199.2 %wgrad.1 = (f32[1536,6144]{1,0:T(8,128)}, f32[6144,1536]{1,0:T(8,128)}) custom-call(f32[4608,4096]{1,0:T(8,128)} %get-tuple-element.25.z_hbm, bf16[6144,1536]{1,0:T(8,128)(2,1)} %bitcast.14, bf16[4,4,2,128,1536]{4,3,2,1,0:T(8,128)(2,1)} %get-tuple-element.19.h_hbm, bf16[4,4,2,128,1536]{4,3,2,1,0:T(8,128)(2,1)} %get-tuple-element.20.g_hbm), custom_call_target="tpu_custom_call" | custom-call | flops 231928233984 | bytes 220200960 | tf_op jit(solution)/shard_map/wgrad/pallas_call | solution.py:561
  461.8 0.0 all-gather.3.cloned.1.call-done.s1
  461.8 0.0 all-gather.5.cloned.1.call-done.s2
  461.9 14.6 %finish.1 = (f32[1536,6144]{1,0:T(8,128)}, f32[6144,1536]{1,0:T(8,128)}) custom-call(f32[1536,1536]{1,0:T(8,128)} %all-gather.3.cloned.1.call-done.s1, f32[1536,1536]{1,0:T(8,128)} %all-gather.5.cloned.1.call-done.s2, f32[1536,6144]{1,0:T(8,128)} %get-tuple-element.26.dw1_in, ...), custom_call_target="tpu_custom_call", output_to_operand_aliasing={{0}: (2, {}), {1}: (3, {})} | custom-call | flops 2359296 | bytes 37748736 | tf_op jit(solution)/shard_map/finish/pallas_call | solution.py:648
Async XLA Ops:
  7.2 454.7 %all-gather.3.cloned.1.call-start = ((), (), s32[]{:S(2)}) async-start(), calls=%async_computation | async-start | bytes 10027008 | tf_op jit(solution)/shard_map/all_gather | solution.py:669
  261.8 200.0 %all-gather.5.cloned.1.call-start = ((), (), s32[]{:S(2)}) async-start(), calls=%async_computation.1 | async-start | bytes 10027008 | tf_op jit(solution)/shard_map/all_gather | solution.py:670
Sparse Core Ops, SparseCore 0:
  262.0 77.4 all-gather.2
  341.6 75.1 all-gather.4
